TPU v7x, 512 devices: a whole 4x8x8 slice. The times are simulated.
512 devices in a mesh: state: 8 (over y_lo, x), bond: 64 (over z, y_hi, core).
Axes of the slice: x: 4, y: 8 (y_hi: 4, y_lo: 2; y = y_hi * 2 + y_lo), z: 8, core: 2. Of those that a mesh axis runs over, the one named last changes fastest.
Arguments:
- intersect_left: bfloat16 [8, 2048, 2048], P('state', 'bond'), may hold values from -0.125 to 0.125
- stored_block: bfloat16 [8, 4, 2048, 2048], P('state', None, 'bond'), may hold values from -6 to 6
- stored_site: bfloat16 [8, 2, 2048, 2048], P('state', None, 'bond'), may hold values from -6 to 6
- current_site: bfloat16 [2048, 2, 2048], P('bond', None, 'state'), may hold values from -0.09375 to 0.09375
- current_block: bfloat16 [4, 2048, 2048], P(None, 'bond', 'state'), may hold values from -6 to 6
- penalty_weight: float32 [8], replicated, may hold values from 0.5 to 4
Outputs:
- penalized: float32 [4, 2048, 2048], P(None, 'bond', 'state')
- intersect_next: bfloat16 [8, 2048, 2048], P('state', 'bond')
All inputs are finite; a program needn't handle non-finite values.
Results may differ from a plain program's by a relative error of at most 0.0055.
Values may be sent and summed in bfloat16 or wider, within the bound.
A program may use at most 64 MiB of HBM per device.

v0:
```python
import jax
import jax.numpy as jnp
from jax import lax
from jax.sharding import Mesh
from jax.sharding import PartitionSpec as P

BOND = ("bond_0", "bond_1", "bond_2")


def laid_out(blocks, dim):
    blocks = jnp.moveaxis(blocks, 0, dim)
    dims = blocks.shape
    return blocks.reshape(*dims[:dim], dims[dim] * dims[dim + 1], *dims[dim + 2 :])


def sent_to_all(value, axis):
    copies = jnp.broadcast_to(value, (lax.axis_size(axis), *value.shape))
    return lax.all_to_all(copies, axis, split_axis=0, concat_axis=0, tiled=True)


def gathered_copies(value, axis, dim):
    return laid_out(sent_to_all(value, axis), dim)


def of_everyone(value, axis):
    return sent_to_all(value, axis).sum(axis=0)


def split_up(value, dim, length):
    dims = value.shape
    blocks = value.reshape(*dims[:dim], length, dims[dim] // length, *dims[dim + 1 :])
    return jnp.moveaxis(blocks, dim, 0)


def sent_and_summed(value, axis, dim):
    length = lax.axis_size(axis)
    blocks = lax.all_to_all(split_up(value, dim, length), axis, 0, 0, tiled=True)
    return jnp.sum(blocks, axis=0)


def gather_in_order(value, axes, sequence):
    blocks = value[None]
    for k in sequence:
        blocks = lax.all_gather(blocks, axes[k], axis=0, tiled=True)
    current = [lax.axis_size(axes[k]) for k in reversed(sequence)]
    blocks = blocks.reshape(*current, *value.shape)
    turned = sorted(range(len(sequence)), key=lambda place: sequence[len(sequence) - 1 - place])
    return blocks.transpose(*turned, *range(len(sequence), blocks.ndim)).reshape(-1, *value.shape)


def whole_of(value, axes, sequence, dim):
    return laid_out(gather_in_order(value, axes, sequence), dim)


def contract_last(left, right):
    return lax.dot_general(
        left, right, (((1,), (1,)), ((), ())), preferred_element_type=jnp.float32
    )


def shards(intersect_left, stored_block, stored_site, current_site, current_block, penalty_weight):
    bond_width = intersect_left.shape[2]
    column_count = stored_block.shape[2]
    pair_count = stored_block.shape[1]
    physical = stored_site.shape[1]
    operand = jnp.concatenate(
        [
            stored_block[0].reshape(pair_count * column_count, bond_width),
            stored_site[0].reshape(physical * column_count, bond_width),
        ],
        axis=0,
    )
    products = contract_last(operand, lax.all_gather(intersect_left, BOND, axis=1, tiled=True)[0])
    projected = products[: pair_count * column_count].reshape(pair_count, column_count, bond_width)
    moved = (
        products[pair_count * column_count :]
        .astype(jnp.bfloat16)
        .reshape(1, physical, column_count, bond_width)
    )
    scale_factor = 1.0 / (physical * bond_width)
    whole_block = gathered_copies(current_block, "state", 2)
    intersect = (
        of_everyone(jnp.sum(projected * whole_block.astype(jnp.float32)), BOND) * scale_factor
    )
    weight = penalty_weight[lax.axis_index("state")]
    summed = sent_and_summed(weight * intersect * projected, "state", 2)
    penalized = current_block.astype(jnp.float32) + summed
    moved_all = gathered_copies(moved, "state", 0)
    grown = jnp.einsum(
        "asf,ksea->kfe",
        whole_of(current_site, BOND, (1, 0, 2), 0),
        moved_all,
        preferred_element_type=jnp.float32,
    )
    intersect_next = lax.all_to_all(
        lax.all_to_all(
            grown.astype(jnp.bfloat16), "state", split_axis=0, concat_axis=1, tiled=True
        ),
        BOND,
        split_axis=1,
        concat_axis=2,
        tiled=True,
    )
    return (penalized, intersect_next)


def solution(mesh):
    torus = Mesh(
        mesh.devices.reshape(mesh.shape["state"], 8, 4, 2), ("state", "bond_0", "bond_1", "bond_2")
    )
    in_specs = (
        P("state", BOND, None),
        P("state", None, BOND, None),
        P("state", None, BOND, None),
        P(BOND, None, "state"),
        P(None, BOND, "state"),
        P(),
    )
    out_specs = (P(None, BOND, "state"), P("state", BOND, None))
    return jax.shard_map(
        shards, mesh=torus, in_specs=in_specs, out_specs=out_specs, check_vma=False
    )
```

profile of v0, /device:TPU:1, one launch (start us, length us, event | category | flops | bytes accessed | tf_op | source)
XLA Modules:
  0.0 254.4 jit_solution(17386184669337860145)
XLA Ops:
  7.2 0.0 all-gather.5.cloned.1.call-start
  7.2 0.7 all-gather.5.cloned.1.call-update
  7.9 1.7 broadcast_in_dim.12
  9.6 5.9 %all-to-all-start = ((bf16[8,4,32,256]{3,2,1,0:T(8,128)(2,1)}), bf16[8,4,32,256]{3,2,1,0:T(8,128)(2,1)S(1)}, u32[]{:S(2)}, u32[]{:S(2)}) async-start(bf16[8,4,32,256]{3,2,1,0:T(8,128)(2,1)} %broadcast_in_dim.12), calls=%async_computation | async-start | bytes 1048576 | tf_op jit(solution)/shard_map/all_to_all | solution.py:18
  15.5 0.0 all-gather.7.cloned.1.call-start
  15.5 0.8 copy.37
  16.3 15.3 %all-gather = bf16[128,2,256]{2,0,1:T(8,128)(2,1)} all-gather(bf16[32,2,256]{2,0,1:T(8,128)(2,1)S(1)} %copy.37), channel_id=2, replica_groups=mesh['state'=8,'bond_0'=8,'bond_1'=4,'bond_2'=2] {'bond_1'}, dimensions={0}, use_global_device_ids=true | all-gather | bytes 163840 | tf_op jit(solution)/shard_map/all_gather | solution.py:44
  31.5 0.0 all-gather.7.cloned.1.call-update
  31.5 0.0 all-to-all-done
  31.6 0.1 convert_bitcast_fusion
  31.7 0.0 copy-start.1
  31.7 0.0 copy-start.2
  31.7 0.6 copy.34
  32.3 0.3 copy.47
  32.7 88.6 %all-gather.5.cloned.1.call-done = bf16[1,2048,2048]{2,1,0:T(8,128)(2,1)} async-done(((bf16[1,32,2048]{2,1,0:T(8,128)(2,1)}), bf16[1,2048,2048]{2,1,0:T(8,128)(2,1)}) %all-gather.5.cloned.1.call-update) | async-done | bytes 8388624 | tf_op jit(solution)/shard_map/all_gather | solution.py:73
  121.3 0.0 copy-done.1
  121.3 0.0 copy-done.2
  121.3 6.3 %fusion = f32[192,2048]{1,0:T(8,128)S(1)} fusion(bf16[1,2048,2048]{2,1,0:T(8,128)(2,1)} %all-gather.5.cloned.1.call-done, bf16[64,2048]{1,0:T(8,128)(2,1)S(1)} %bitcast.65, bf16[128,2048]{1,0:T(8,128)(2,1)S(1)} %bitcast.64), kind=kOutput, calls=%fused_computation | convolution fusion | flops 1612185600 | bytes 10747904 | tf_op jit(solution)/shard_map/dot_general | solution.py:56
  127.5 0.9 multiply_reduce_fusion
  128.4 1.3 broadcast_in_dim.13
  129.7 7.3 %all-to-all-start.1 = ((f32[64,1,1]{2,1,0:T(1,128)}), f32[64,1,1]{2,1,0:T(1,128)S(1)}, u32[]{:S(2)}, u32[]{:S(2)}) async-start(f32[64,1,1]{2,1,0:T(1,128)} %broadcast_in_dim.13), calls=%async_computation.1 | async-start | bytes 65536 | tf_op jit(solution)/shard_map/all_to_all | solution.py:18
  137.1 11.7 %all-to-all-done.1 = f32[64,1,1]{2,1,0:T(1,128)S(1)} async-done(((f32[64,1,1]{2,1,0:T(1,128)}), f32[64,1,1]{2,1,0:T(1,128)S(1)}, u32[]{:S(2)}, u32[]{:S(2)}) %all-to-all-start.1) | async-done | bytes 288 | tf_op jit(solution)/shard_map/all_to_all | solution.py:18
  148.8 1.6 broadcast_in_dim.14
  150.3 0.0 copy-start.3
  150.3 4.5 %all-to-all-start.3 = ((bf16[8,1,2,32,2048]{4,3,2,1,0:T(8,128)(2,1)}), bf16[8,1,2,32,2048]{4,3,2,1,0:T(8,128)(2,1)}, u32[]{:S(2)}, u32[]{:S(2)}) async-start(bf16[8,1,2,32,2048]{4,3,2,1,0:T(8,128)(2,1)} %broadcast_in_dim.14), calls=%async_computation.3 | async-start | bytes 4194304 | tf_op jit(solution)/shard_map/all_to_all | solution.py:18
  154.9 0.0 all-gather.9.cloned.1.call-start
  154.9 1.0 all-gather.7.cloned.1.call-done
  155.9 0.0 all-gather.9.cloned.1.call-update
  156.0 0.0 copy-done.3
  156.0 0.6 dynamic_slice.3
  156.6 24.2 %all-gather.9.cloned.1.call-done = bf16[64,32,2,256]{3,1,0,2:T(8,128)(2,1)} async-done(((bf16[32,32,2,256]{3,1,0,2:T(8,128)(2,1)}), bf16[64,32,2,256]{3,1,0,2:T(8,128)(2,1)}) %all-gather.9.cloned.1.call-update) | async-done | bytes 2097168 | tf_op jit(solution)/shard_map/all_gather | solution.py:44
  180.8 3.2 %copy.39 = bf16[8,4,2,32,2,256]{5,3,2,1,0,4:T(8,128)(2,1)} copy(bf16[8,4,2,32,2,256]{5,3,1,0,2,4:T(8,128)(2,1)} %bitcast.60) | data formatting | bytes 4194304 | tf_op jit(solution)/shard_map/transpose | solution.py:48
  184.0 0.7 reduce_sum.28
  185.9 0.0 all-to-all-done.3
  185.9 3.6 %fusion.10 = bf16[8,256,32]{1,2,0:T(8,128)(2,1)} fusion(bf16[2048,2,256,1]{2,0,1,3:T(8,128)(2,1)} %bitcast.61, bf16[8,1,2,32,2048]{4,3,2,1,0:T(8,128)(2,1)} %all-to-all-done.3), kind=kOutput, calls=%fused_computation.6 | convolution fusion | flops 536936448 | bytes 4325376 | tf_op jit(solution)/shard_map/asf,ksea->kfe/dot_general | solution.py:89
  189.5 3.9 %all-to-all-start.4 = ((bf16[8,256,32]{1,2,0:T(8,128)(2,1)}), bf16[8,256,32]{1,2,0:T(8,128)(2,1)S(1)}, u32[]{:S(2)}, u32[]{:S(2)}) async-start(bf16[8,256,32]{1,2,0:T(8,128)(2,1)} %fusion.10), calls=%async_computation.4 | async-start | bytes 262144 | tf_op jit(solution)/shard_map/all_to_all | solution.py:96
  193.4 0.1 slice_multiply_fusion
  193.5 0.3 copy.48
  193.9 1.3 copy.50
  195.2 3.9 %all-to-all-done.4 = bf16[8,256,32]{1,2,0:T(8,128)(2,1)S(1)} async-done(((bf16[8,256,32]{1,2,0:T(8,128)(2,1)}), bf16[8,256,32]{1,2,0:T(8,128)(2,1)S(1)}, u32[]{:S(2)}, u32[]{:S(2)}) %all-to-all-start.4) | async-done | bytes 131104 | tf_op jit(solution)/shard_map/all_to_all | solution.py:96
  199.0 3.7 %all-to-all-start.2 = ((f32[8,4,32,256]{3,2,1,0:T(8,128)}), f32[8,4,32,256]{3,2,1,0:T(8,128)S(1)}, u32[]{:S(2)}, u32[]{:S(2)}) async-start(f32[8,4,32,256]{3,2,1,0:T(8,128)} %bitcast.52), calls=%async_computation.2 | async-start | bytes 2097152 | tf_op jit(solution)/shard_map/all_to_all | solution.py:37
  202.8 0.1 copy.40
  202.9 0.1 all_to_all.40
  202.9 0.7 copy.41
  203.7 0.0 copy-start
  203.7 0.5 broadcast.5
  204.2 11.5 %reduce.2 = bf16[2048,32]{1,0:T(8,128)(2,1)S(1)} reduce(bf16[2048,1,32]{2,1,0:T(2,128)(2,1)S(1)} %bitcast.56, bf16[]{:T(256)} %broadcast.5), dimensions={1}, to_apply=%bitcast.49.reduce_sub_computation | reduce | bytes 262146
  215.7 1.1 reshape.36
  216.8 0.0 all-to-all-done.2
  216.8 13.4 %all-to-all-start.5 = ((bf16[64,2,512]{2,1,0:T(2,128)(2,1)}), bf16[64,2,512]{2,1,0:T(2,128)(2,1)S(1)}, u32[]{:S(2)}, u32[]{:S(2)}) async-start(bf16[64,2,512]{2,1,0:T(2,128)(2,1)} %reshape.36), calls=%async_computation.5 | async-start | bytes 262144 | tf_op jit(solution)/shard_map/all_to_all | solution.py:95
  230.2 0.1 reduce_sum.29
  230.3 0.0 copy-done
  230.3 0.7 convert_add_fusion
  231.0 13.0 %all-to-all-done.5 = bf16[64,2,512]{2,1,0:T(2,128)(2,1)S(1)} async-done(((bf16[64,2,512]{2,1,0:T(2,128)(2,1)}), bf16[64,2,512]{2,1,0:T(2,128)(2,1)S(1)}, u32[]{:S(2)}, u32[]{:S(2)}) %all-to-all-start.5) | async-done | bytes 131104 | tf_op jit(solution)/shard_map/all_to_all | solution.py:95
  244.0 0.7 reshape.37
  244.6 0.5 copy.42
  245.2 0.4 all_to_all.42
  245.6 1.1 copy.43
  246.7 1.2 all_to_all.44
  (1 shorter events, 0.0 us)
Async XLA Ops:
  7.2 114.1 %all-gather.5.cloned.1.call-start = ((), (), s32[]{:S(2)}) async-start(), calls=%async_computation.6 | async-start | bytes 8519680 | tf_op jit(solution)/shard_map/all_gather | solution.py:73
  9.6 21.9 %all-to-all-start = ((bf16[8,4,32,256]{3,2,1,0:T(8,128)(2,1)}), bf16[8,4,32,256]{3,2,1,0:T(8,128)(2,1)S(1)}, u32[]{:S(2)}, u32[]{:S(2)}) async-start(bf16[8,4,32,256]{3,2,1,0:T(8,128)(2,1)} %broadcast_in_dim.12), calls=%async_computation | async-start | bytes 1048576 | tf_op jit(solution)/shard_map/all_to_all | solution.py:18
  15.5 140.5 %all-gather.7.cloned.1.call-start = ((), (), s32[]{:S(2)}) async-start(), calls=%async_computation.7 | async-start | bytes 1179648 | tf_op jit(solution)/shard_map/all_gather | solution.py:44
  31.7 89.6 %copy-start.1 = (bf16[1,4,32,2048]{3,2,1,0:T(8,128)(2,1)S(1)}, bf16[1,4,32,2048]{3,2,1,0:T(8,128)(2,1)}, u32[]{:S(2)}) copy-start(bf16[1,4,32,2048]{3,2,1,0:T(8,128)(2,1)} %param.7) | copy-start | bytes 1572868
  31.7 89.6 %copy-start.2 = (bf16[1,2,32,2048]{3,2,1,0:T(8,128)(2,1)S(1)}, bf16[1,2,32,2048]{3,2,1,0:T(8,128)(2,1)}, u32[]{:S(2)}) copy-start(bf16[1,2,32,2048]{3,2,1,0:T(8,128)(2,1)} %param.8) | copy-start | bytes 786436
  129.7 19.0 %all-to-all-start.1 = ((f32[64,1,1]{2,1,0:T(1,128)}), f32[64,1,1]{2,1,0:T(1,128)S(1)}, u32[]{:S(2)}, u32[]{:S(2)}) async-start(f32[64,1,1]{2,1,0:T(1,128)} %broadcast_in_dim.13), calls=%async_computation.1 | async-start | bytes 65536 | tf_op jit(solution)/shard_map/all_to_all | solution.py:18
  150.3 5.6 %copy-start.3 = (f32[8]{0:T(128)S(1)}, f32[8]{0:T(128)}, u32[]{:S(2)}) copy-start(f32[8]{0:T(128)} %param.11) | copy-start | bytes 100
  150.3 35.6 %all-to-all-start.3 = ((bf16[8,1,2,32,2048]{4,3,2,1,0:T(8,128)(2,1)}), bf16[8,1,2,32,2048]{4,3,2,1,0:T(8,128)(2,1)}, u32[]{:S(2)}, u32[]{:S(2)}) async-start(bf16[8,1,2,32,2048]{4,3,2,1,0:T(8,128)(2,1)} %broadcast_in_dim.14), calls=%async_computation.3 | async-start | bytes 4194304 | tf_op jit(solution)/shard_map/all_to_all | solution.py:18
  154.9 25.9 %all-gather.9.cloned.1.call-start = ((), (), s32[]{:S(2)}) async-start(), calls=%async_computation.8 | async-start | bytes 3145728 | tf_op jit(solution)/shard_map/all_gather | solution.py:44
  189.5 9.5 %all-to-all-start.4 = ((bf16[8,256,32]{1,2,0:T(8,128)(2,1)}), bf16[8,256,32]{1,2,0:T(8,128)(2,1)S(1)}, u32[]{:S(2)}, u32[]{:S(2)}) async-start(bf16[8,256,32]{1,2,0:T(8,128)(2,1)} %fusion.10), calls=%async_computation.4 | async-start | bytes 262144 | tf_op jit(solution)/shard_map/all_to_all | solution.py:96
  199.0 17.8 %all-to-all-start.2 = ((f32[8,4,32,256]{3,2,1,0:T(8,128)}), f32[8,4,32,256]{3,2,1,0:T(8,128)S(1)}, u32[]{:S(2)}, u32[]{:S(2)}) async-start(f32[8,4,32,256]{3,2,1,0:T(8,128)} %bitcast.52), calls=%async_computation.2 | async-start | bytes 2097152 | tf_op jit(solution)/shard_map/all_to_all | solution.py:37
  203.7 26.6 %copy-start = (bf16[4,32,256]{2,1,0:T(8,128)(2,1)S(1)}, bf16[4,32,256]{2,1,0:T(8,128)(2,1)}, u32[]{:S(2)}) copy-start(bf16[4,32,256]{2,1,0:T(8,128)(2,1)} %param.10) | copy-start | bytes 196612
  216.8 27.1 %all-to-all-start.5 = ((bf16[64,2,512]{2,1,0:T(2,128)(2,1)}), bf16[64,2,512]{2,1,0:T(2,128)(2,1)S(1)}, u32[]{:S(2)}, u32[]{:S(2)}) async-start(bf16[64,2,512]{2,1,0:T(2,128)(2,1)} %reshape.36), calls=%async_computation.5 | async-start | bytes 262144 | tf_op jit(solution)/shard_map/all_to_all | solution.py:95
Sparse Core Ops, SparseCore 0:
  11.3 109.8 all-gather.4
  123.3 32.5 all-gather.6
  158.0 22.6 all-gather.8
where the time goes:
time: 255 us; the launch traced here: 254 us
  waiting for transfers between devices  143 us (56%)
  starting transfers between devices  38.8 us (15%)
  local copies, waits for them, and re-layouts  18.1 us (7%)
  blocking collectives  15.3 us (6%)
  between operations  15.2 us (6%)
  other arithmetic  14 us (5%)
  matrix products  9.87 us (4%)
    all_gather x1, waiting for transfers between devices, shards(): lax.all_gather(intersect_left, BOND, axis=1, tiled=True)[0]  88.6 us
    all_gather x2, waiting for transfers between devices, gather_in_order(): blocks = lax.all_gather(blocks, axes[k], axis=0, tiled=True)  25.2 us
    all_to_all x3, starting transfers between devices, sent_to_all(): return lax.all_to_all(copies, axis, split_axis=0, concat_axis=0, tiled=True)  17.7 us
    all_gather x1, blocking collectives, gather_in_order(): blocks = lax.all_gather(blocks, axes[k], axis=0, tiled=True)  15.3 us
    all_to_all x1, starting transfers between devices, shards(): lax.all_to_all(lax.all_to_all(grown.astype(jnp.bfloat16), 'state', split_...  13.4 us
    all_to_all x1, waiting for transfers between devices, shards(): lax.all_to_all(lax.all_to_all(grown.astype(jnp.bfloat16), 'state', split_...  13 us
    all_to_all x3, waiting for transfers between devices, sent_to_all(): return lax.all_to_all(copies, axis, split_axis=0, concat_axis=0, tiled=True)  11.7 us
    unnamed x1, other arithmetic  11.5 us
  transfers between devices with their start and end apart: 9, of which 6 were waited for; matrix products, arithmetic and copies ran while one was open for 14% of the time, Pallas kernels for 0%

commit v1 on v0

v1 whole, which is shorter than its diff:
```python
import functools

import jax
import jax.numpy as jnp
from jax import lax
from jax.experimental import pallas as pl
from jax.experimental.pallas import tpu as pltpu
from jax.sharding import Mesh
from jax.sharding import PartitionSpec as P

BF = jnp.bfloat16
F32 = jnp.float32
STATE = ("yl", "x")
BOND = ("z", "yh", "c")
TURN = (0, 1, 3, 2)
WIDE = 2048
SITE = 512
COLS = WIDE + SITE

COMMON = [
    (0, 0), (1, 0), (0, 1), (0, 2), (2, 0), (0, 3),
    (1, 1), (1, 2), (1, 3), (2, 1), (2, 2), (2, 3),
]
UP_ORDER = COMMON + [(3, 0), (3, 1), (3, 2), (3, 3)]
DOWN_ORDER = COMMON + [(3, 2), (3, 3), (3, 0), (3, 1)]


def slot_up(s):
    return 0 if s == 0 else (7 if s == 4 else 2 * s - 1)


def slot_down(s):
    return 0 if s == 0 else (7 if s == 4 else 2 * s)


def remote(src, dst, send, recv, device):
    return pltpu.make_async_remote_copy(
        src_ref=src, dst_ref=dst, send_sem=send, recv_sem=recv,
        device_id=device, device_id_type=pl.DeviceIdType.MESH,
    )


def lanes_to_halves(low, high):
    lane = lax.broadcasted_iota(jnp.int32, low.shape, 1) // 32
    first = jnp.where(lane == 0, low, jnp.where(lane == 1, pltpu.roll(low, 96, 1),
                      jnp.where(lane == 2, pltpu.roll(high, 64, 1), pltpu.roll(high, 32, 1))))
    second = jnp.where(lane == 0, pltpu.roll(low, 96, 1), jnp.where(lane == 1, pltpu.roll(low, 64, 1),
                       jnp.where(lane == 2, pltpu.roll(high, 32, 1), high)))
    return first, second


def halves_to_lanes(first, second):
    lane = lax.broadcasted_iota(jnp.int32, first.shape, 1) // 32
    low = jnp.where(lane == 0, first, jnp.where(lane == 1, pltpu.roll(second, 32, 1),
                    jnp.where(lane == 2, pltpu.roll(first, 32, 1), pltpu.roll(second, 64, 1))))
    high = jnp.where(lane == 0, pltpu.roll(first, 64, 1), jnp.where(lane == 1, pltpu.roll(second, 96, 1),
                     jnp.where(lane == 2, pltpu.roll(first, 96, 1), second)))
    return low, high


def kernel(chunk_ref, block_ref, site_ref, current_ref, weight_ref, pen_ref, next_ref,
           rows, stored, proj_out, proj_in, moved, grown, grown_in, tiles_out, tiles_in, dots,
           local_sem, y_send, y_recv, z_send, z_recv, s_send, s_recv, p_send, p_recv,
           m_send, m_recv, g_send, g_recv, o_send, o_recv, r_send, r_recv):
    yl, x, z, yh, c = (lax.axis_index(n) for n in ("yl", "x", "z", "yh", "c"))
    state = yl * 4 + x
    up = {"z": lax.rem(z + 1, 8)}
    down = {"z": lax.rem(z + 7, 8)}
    sibling = {"c": 1 - c}
    partner = {"yl": 1 - yl}

    def source(q):
        return lax.rem(yh + TURN[q], 4)

    mine = pltpu.make_async_copy(chunk_ref, rows.at[0, yh], local_sem.at[0])
    mine.start()
    own = [
        pltpu.make_async_copy(block_ref.at[0], stored.at[pl.ds(0, 4), c], local_sem.at[1]),
        pltpu.make_async_copy(site_ref.at[0], stored.at[pl.ds(4, 2), c], local_sem.at[2]),
    ]
    for copy in own:
        copy.start()
    swap = [
        remote(block_ref.at[0], stored.at[pl.ds(0, 4), c], s_send.at[0], s_recv.at[0], sibling),
        remote(site_ref.at[0], stored.at[pl.ds(4, 2), c], s_send.at[1], s_recv.at[1], sibling),
    ]
    mine.wait()

    def pass_up(s, q):
        block = source(q)
        return remote(rows.at[slot_up(s), block], rows.at[slot_up(s + 1), block],
                      z_send, z_recv.at[0, s + 1, q], up)

    def pass_down(s, q):
        block = source(q)
        return remote(rows.at[slot_down(s), block], rows.at[slot_down(s + 1), block],
                      z_send, z_recv.at[1, s + 1, q], down)

    def give(q):
        return remote(rows.at[0, yh], rows.at[0, yh], y_send, y_recv.at[q],
                      {"yh": lax.rem(yh + 4 - TURN[q], 4)})

    pass_up(0, 0).start()
    pass_down(0, 0).start()
    for q in (1, 2, 3):
        give(q).start()
    for copy in swap:
        copy.start()

    low, high = (current_ref[:, :, 128 * h:128 * (h + 1)].astype(F32).reshape(128, 128) for h in (0, 1))
    current = lanes_to_halves(low, high)

    for copy in own:
        copy.wait()
    for copy in swap:
        copy.wait_recv()
    grown[...] = jnp.zeros_like(grown)

    def row_of(t):
        if t == 7:
            return lax.rem(z + 4, 8)
        d = (t + 1) // 2
        return lax.rem(z + (8 - d if t % 2 else d), 8)

    def to_state(t, same):
        r = row_of(t)
        core = c if same else 1 - c
        return remote(proj_out.at[t, core], proj_in.at[state, c], p_send, p_recv.at[state, c],
                      {"yl": r // 4, "x": lax.rem(r, 4), "c": core})

    def moved_copy(t, other, device, sem):
        k = (1 - yl if other else yl) * 4 + x
        return remote(moved.at[t, k], moved.at[t, k], m_send, m_recv.at[t, sem], device)

    def along_x(t, other):
        return [moved_copy(t, other, {"x": lax.rem(x + o, 4)}, (4 if other else 0) + o) for o in (1, 2, 3)]

    def multiply(t):
        left = stored[...].reshape(384, WIDE)
        right = rows[t, :, :, 0:WIDE].reshape(128, WIDE)
        product = lax.dot_general(left, right, (((1,), (1,)), ((), ())), preferred_element_type=F32).astype(BF)
        blocks = product[0:256].reshape(4, 2, 32, 128)
        for j in (0, 1):
            proj_out[t, j] = blocks[:, j].reshape(128, 128)
        moved[t, state] = product[256:384]
        moved_copy(t, False, partner, 4).start()
        for copy in along_x(t, False):
            copy.start()
        home = row_of(t) == state

        @pl.when(home)
        def _():
            proj_in[state, c] = proj_out[t, c]

        @pl.when(jnp.logical_not(home))
        def _():
            to_state(t, True).start()

        to_state(t, False).start()

    def relay(t):
        moved_copy(t, False, partner, 4).wait_recv()
        for copy in along_x(t, True):
            copy.start()

    def grow(t):
        for other in (False, True):
            for copy in along_x(t, other):
                copy.wait_recv()
        for s in (0, 1):
            site = rows[t, :, :, WIDE + 256 * s:WIDE + 256 * (s + 1)].reshape(128, 256)
            right = moved[t, :, 64 * s:64 * (s + 1), :].reshape(512, 128)
            grown[...] += lax.dot_general(site, right, (((0,), (1,)), ((), ())), preferred_element_type=F32)

    done = []

    def step(t):
        multiply(t)
        done.append(t)
        if len(done) >= 2:
            relay(done[-2])
        if len(done) >= 4:
            grow(done[-4])

    for place in range(16):
        for order, passing, lane, last in ((UP_ORDER, pass_up, 0, (0, 1)), (DOWN_ORDER, pass_down, 1, (2, 3))):
            s, q = order[place]
            if s == 0:
                if lane == 0 and q > 0:
                    give(q).wait_recv()
            else:
                passing(s - 1, q).wait_recv()
            if (s, q) != (0, 0) and (s < 3 or q in last):
                passing(s, q).start()
        s, q = UP_ORDER[place]
        if q == 3:
            if s == 0:
                step(0)
            else:
                step(slot_up(s))
                step(slot_down(s))
    for q in (0, 1):
        pass_up(3, q).wait_recv()
    for q in (2, 3):
        pass_down(3, q).wait_recv()
    multiply(7)
    relay(6)
    relay(7)
    for t in done[-3:]:
        grow(t)

    for k in range(8):
        for i in (0, 1):
            @pl.when(jnp.logical_or(k != state, i != c))
            def _():
                pltpu.make_async_copy(proj_in.at[k, i], proj_in.at[k, i], p_recv.at[k, i]).wait()
    partial = [
        sum(jnp.sum((proj_in[k, i].astype(F32) * current[i]).reshape(16, 8, 128), axis=0) for i in (0, 1))
        for k in range(8)
    ]
    partial = jnp.concatenate([jnp.sum(p, axis=0, keepdims=True) for p in partial], axis=0)

    places = (x * 2 + c, z, yl * 4 + yh)

    def peer(stage, o):
        there = lax.rem(places[stage] + o, 8)
        if stage == 0:
            return {"x": there // 2, "c": lax.rem(there, 2)}
        if stage == 1:
            return {"z": there}
        return {"yl": there // 4, "yh": lax.rem(there, 4)}

    def exchange(stage, value):
        dots[stage, places[stage]] = value
        for o in range(1, 8):
            here = dots.at[stage, places[stage]]
            remote(here, here, r_send.at[stage], r_recv.at[stage], peer(stage, o)).start()

    def collected(stage):
        seven = dots.at[stage, pl.ds(0, 7)]
        pltpu.make_async_copy(seven, seven, r_recv.at[stage]).wait()
        return jnp.sum(dots[stage], axis=0)

    exchange(0, partial)
    grow(7)
    give_half = remote(grown.at[pl.ds(128 * (1 - c), 128)], grown_in, g_send, g_recv, sibling)
    give_half.start()
    exchange(1, collected(0))
    give_half.wait_recv()

    lane = lax.broadcasted_iota(jnp.int32, (16, 128), 1)
    half = grown.at[pl.ds(pl.multiple_of(128 * c, 128), 128)]
    for d in range(4):
        for pair in range(4):
            cut = pl.ds(128 * pair, 128)
            first = half[pl.ds(32 * d, 16), cut] + grown_in[pl.ds(32 * d, 16), cut]
            second = half[pl.ds(32 * d + 16, 16), cut] + grown_in[pl.ds(32 * d + 16, 16), cut]
            tiles_out[2 * pair, d] = jnp.where(lane < 64, first, pltpu.roll(second, 64, 1)).astype(BF)
            tiles_out[2 * pair + 1, d] = jnp.where(lane < 64, pltpu.roll(first, 64, 1), second).astype(BF)

    place = z * 4 + yh
    for k in range(8):
        for d in range(4):
            to = 2 * c + d // 2
            here = jnp.logical_and(jnp.logical_and(k == state, z == state), jnp.logical_and(to == yh, d % 2 == c))

            @pl.when(here)
            def _():
                pltpu.make_async_copy(tiles_out.at[k, d], tiles_in.at[place], o_recv).start()

            @pl.when(jnp.logical_not(here))
            def _():
                remote(tiles_out.at[k, d], tiles_in.at[place], o_send, o_recv,
                       {"yl": k // 4, "x": k % 4, "z": state, "yh": to, "c": d % 2}).start()

    exchange(2, collected(1))
    total = jnp.sum(collected(2), axis=1, keepdims=True) * (1.0 / 4096.0)
    factor = total * weight_ref[...]
    halves = []
    for i in (0, 1):
        value = current[i]
        for k in range(8):
            value = value + factor[k:k + 1, :] * proj_in[k, i].astype(F32)
        halves.append(value)
    low, high = halves_to_lanes(*halves)
    pen_ref[:, :, 0:128] = low.reshape(4, 32, 128)
    pen_ref[:, :, 128:256] = high.reshape(4, 32, 128)

    pltpu.make_async_copy(tiles_in, tiles_in, o_recv).wait()
    for p in range(16):
        even = tiles_in[2 * p].astype(F32)
        odd = tiles_in[2 * p + 1].astype(F32)
        cut = slice(128 * p, 128 * (p + 1))
        next_ref[0, 0:16, cut] = jnp.where(lane < 64, even, pltpu.roll(odd, 64, 1)).astype(BF)
        next_ref[0, 16:32, cut] = jnp.where(lane < 64, pltpu.roll(even, 64, 1), odd).astype(BF)

    def drained(ref, sem):
        pltpu.make_async_copy(ref, ref, sem).wait()

    for copy in swap:
        copy.wait_send()
    drained(rows.at[0, pl.ds(0, 3)], y_send)
    drained(rows.at[pl.ds(0, 7)], z_send)
    drained(proj_in.at[pl.ds(0, 7)], p_send)
    drained(proj_in.at[0, 0], p_send)
    drained(moved.at[pl.ds(0, 7)], m_send)
    give_half.wait_send()
    for stage in range(3):
        drained(dots.at[stage, pl.ds(0, 7)], r_send.at[stage])
    drained(tiles_in.at[pl.ds(0, 31)], o_send)

    @pl.when(jnp.logical_not(jnp.logical_and(z == state, yh // 2 == c)))
    def _():
        drained(tiles_in.at[0], o_send)


def shards(intersect_left, stored_block, stored_site, current_site, current_block, penalty_weight):
    chunk = jnp.concatenate([intersect_left[0], current_site.reshape(32, SITE)], axis=1)
    weight = jnp.broadcast_to(penalty_weight[:, None], (8, 128))
    hbm = pl.BlockSpec(memory_space=pl.ANY)
    vmem = pl.BlockSpec(memory_space=pltpu.VMEM)
    dma = pltpu.SemaphoreType.DMA
    return pl.pallas_call(
        kernel,
        out_shape=(
            jax.ShapeDtypeStruct((4, 32, 256), F32),
            jax.ShapeDtypeStruct((1, 32, 2048), BF),
        ),
        in_specs=[hbm, hbm, hbm, vmem, vmem],
        out_specs=(vmem, vmem),
        scratch_shapes=[
            pltpu.VMEM((8, 4, 32, COLS), BF),
            pltpu.VMEM((6, 2, 32, WIDE), BF),
            pltpu.VMEM((8, 2, 128, 128), BF),
            pltpu.VMEM((8, 2, 128, 128), BF),
            pltpu.VMEM((8, 8, 128, 128), BF),
            pltpu.VMEM((256, 512), F32),
            pltpu.VMEM((128, 512), F32),
            pltpu.VMEM((8, 4, 16, 128), BF),
            pltpu.VMEM((32, 16, 128), BF),
            pltpu.VMEM((3, 8, 8, 128), F32),
            dma((3,)), dma, dma((4,)), dma, dma((2, 5, 4)), dma((2,)), dma((2,)), dma, dma((8, 2)),
            dma, dma((8, 8)), dma, dma, dma, dma, dma((3,)), dma((3,)),
        ],
        compiler_params=pltpu.CompilerParams(has_side_effects=True, vmem_limit_bytes=48 * 1024 * 1024),
        name="project_and_grow",
    )(chunk, stored_block, stored_site, current_block, weight)


def solution(mesh):
    torus = Mesh(mesh.devices.reshape(2, 4, 8, 4, 2), STATE + BOND)
    in_specs = (
        P(STATE, BOND, None),
        P(STATE, None, BOND, None),
        P(STATE, None, BOND, None),
        P(BOND, None, STATE),
        P(None, BOND, STATE),
        P(),
    )
    out_specs = (P(None, BOND, STATE), P(STATE, BOND, None))
    return jax.shard_map(shards, mesh=torus, in_specs=in_specs, out_specs=out_specs, check_vma=False)
```

time: 255 us -> 114 us (0.45)
  waiting for transfers between devices: 143 us -> 0 us
  Pallas kernels: 0 us -> 109 us
  starting transfers between devices: 38.8 us -> 0 us
  blocking collectives: 15.3 us -> 0 us
  between operations: 15.2 us -> 0.68 us
  local copies, waits for them, and re-layouts: 18.1 us -> 3.89 us
  other arithmetic: 14 us -> 0.95 us
  matrix products: 9.87 us -> 0 us
    all_gather x3 -> x0, waiting for transfers between devices: 114 us -> none  [the longest x1 88.6 us: shards(): lax.all_gather(intersect_left, BOND, axis=1, tiled=True)[0]]
    pallas_call x0 -> x1, Pallas kernels: none -> 109 us  [shards(): pl.pallas_call(kernel, out_shape=(jax.ShapeDtypeStruct((4, 32, 256), F32)...]
    all_to_all x6 -> x0, starting transfers between devices: 38.7 us -> none  [the longest x3 17.7 us: sent_to_all(): return lax.all_to_all(copies, axis, split_axis=0, concat_axis=0, tiled=True)]
    all_to_all x6 -> x0, waiting for transfers between devices: 28.5 us -> none  [the longest x1 13 us: shards(): lax.all_to_all(lax.all_to_all(grown.astype(jnp.bfloat16), 'state', split_...]
    all_gather x1 -> x0, blocking collectives: 15.3 us -> none  [gather_in_order(): blocks = lax.all_gather(blocks, axes[k], axis=0, tiled=True)]
    unnamed x1 -> x0, other arithmetic: 11.5 us -> none
    dot_general x2 -> x0, matrix products: 9.87 us -> none  [the longest x1 6.28 us: contract_last(): lax.dot_general(left, right, (((1,), (1,)), ((), ())), preferred_element_...]
    all_to_all x7 -> x0, local copies, waits for them, and re-layouts: 4.08 us -> none  [the longest x4 3.2 us: shards(): lax.all_to_all(lax.all_to_all(grown.astype(jnp.bfloat16), 'state', split_...]
  transfers between devices with their start and end apart: 9 -> 0, of which waited for: 6 -> 0; matrix products, arithmetic and copies ran while one was open for 14% -> 0% of each run, Pallas kernels for 0% -> 0%
where the time goes in v1:
time: 114 us
  Pallas kernels  109 us (96%)
  local copies, waits for them, and re-layouts  3.89 us (3%)
    pallas_call x1, Pallas kernels, shards(): pl.pallas_call(kernel, out_shape=(jax.ShapeDtypeStruct((4, 32, 256), F32)...  109 us
    unnamed x9, local copies, waits for them, and re-layouts  3.12 us

profile of v1, /device:TPU:1, one launch (start us, length us, event | category | flops | bytes accessed | tf_op | source)
XLA Modules:
  0.0 114.1 jit_solution(4469304948944038172)
XLA Ops:
  0.6 0.0 copy-start.1
  0.6 0.8 broadcast_in_dim.2.weight_ref
  1.4 0.8 copy.8
  2.2 0.0 copy-start.2
  2.2 0.9 pad_maximum_fusion.chunk_ref
  3.1 0.0 copy-done.1
  3.1 0.0 copy-done.2
  3.1 0.0 copy-start
  3.2 1.0 copy-done
  4.2 108.6 %project_and_grow.1 = (f32[4,32,256]{2,1,0:T(8,128)S(1)}, bf16[1,32,2048]{2,1,0:T(8,128)(2,1)S(1)}) custom-call(bf16[32,2560]{1,0:T(8,128)(2,1)S(1)} %pad_maximum_fusion.chunk_ref, bf16[1,4,32,2048]{3,2,1,0:T(8,128)(2,1)S(1)} %copy-done, bf16[1,2,32,2048]{3,2,1,0:T(8,128)(2,1)S(1)} %copy-done.1, bf16[4,32,256]{2,1,0:T(8,128)(2,1)S(1)} %copy-done.2, ...), custom_call_target="tpu_custom_call" | custom-call | tf_op jit(solution)/shard_map/project_and_grow/pallas_call | solution.py:323
  112.8 0.7 copy.11
  113.5 0.7 copy.12
Async XLA Ops:
  0.6 2.5 %copy-start.1 = (bf16[1,2,32,2048]{3,2,1,0:T(8,128)(2,1)S(1)}, bf16[1,2,32,2048]{3,2,1,0:T(8,128)(2,1)}, u32[]{:S(2)}) copy-start(bf16[1,2,32,2048]{3,2,1,0:T(8,128)(2,1)} %site_ref.1) | copy-start | bytes 786436
  2.2 1.0 copy-start.2
  3.1 1.0 copy-start

commit v2 on v1

--- a/solution.py
+++ b/solution.py
@@ -1,5 +1,3 @@
-import functools
-
 import jax
 import jax.numpy as jnp
 from jax import lax
@@ -15,7 +13,6 @@
 TURN = (0, 1, 3, 2)
 WIDE = 2048
 SITE = 512
-COLS = WIDE + SITE
 
 COMMON = [
     (0, 0), (1, 0), (0, 1), (0, 2), (2, 0), (0, 3),
@@ -23,6 +20,8 @@
 ]
 UP_ORDER = COMMON + [(3, 0), (3, 1), (3, 2), (3, 3)]
 DOWN_ORDER = COMMON + [(3, 2), (3, 3), (3, 0), (3, 1)]
+HOPS = {1: 1, 4: 2, 6: 3, 8: 4}
+RELAYS = {3: (0,), 6: (1, 2), 8: (3, 4), 10: (5, 6), 11: (7,)}
 
 
 def slot_up(s):
@@ -58,33 +57,46 @@
     return low, high
 
 
-def kernel(chunk_ref, block_ref, site_ref, current_ref, weight_ref, pen_ref, next_ref,
-           rows, stored, proj_out, proj_in, moved, grown, grown_in, tiles_out, tiles_in, dots,
+def kernel(env_ref, block_ref, site_ref, edge_ref, current_ref, weight_ref, pen_ref, next_ref,
+           rows, stored, edges, now, proj_out, proj_in, moved, grown, grown_in, tiles_out, tiles_in, dots,
            local_sem, y_send, y_recv, z_send, z_recv, s_send, s_recv, p_send, p_recv,
-           m_send, m_recv, g_send, g_recv, o_send, o_recv, r_send, r_recv):
+           m_send, m_recv, g_send, g_recv, o_send, o_recv, r_send, r_recv, e_send, ez_recv, ey_recv):
     yl, x, z, yh, c = (lax.axis_index(n) for n in ("yl", "x", "z", "yh", "c"))
     state = yl * 4 + x
     up = {"z": lax.rem(z + 1, 8)}
     down = {"z": lax.rem(z + 7, 8)}
     sibling = {"c": 1 - c}
     partner = {"yl": 1 - yl}
+    ahead = {"yh": lax.rem(yh + 1, 4)}
+    behind = {"yh": lax.rem(yh + 3, 4)}
 
     def source(q):
         return lax.rem(yh + TURN[q], 4)
 
-    mine = pltpu.make_async_copy(chunk_ref, rows.at[0, yh], local_sem.at[0])
-    mine.start()
     own = [
-        pltpu.make_async_copy(block_ref.at[0], stored.at[pl.ds(0, 4), c], local_sem.at[1]),
-        pltpu.make_async_copy(site_ref.at[0], stored.at[pl.ds(4, 2), c], local_sem.at[2]),
+        pltpu.make_async_copy(env_ref.at[0], rows.at[0, yh], local_sem.at[0]),
+        pltpu.make_async_copy(edge_ref, edges.at[0, yh], local_sem.at[1]),
+        pltpu.make_async_copy(block_ref.at[0], stored.at[pl.ds(0, 4), c], local_sem.at[2]),
+        pltpu.make_async_copy(site_ref.at[0], stored.at[pl.ds(4, 2), c], local_sem.at[3]),
+        pltpu.make_async_copy(current_ref, now, local_sem.at[4]),
     ]
     for copy in own:
         copy.start()
+
+    barrier = pltpu.get_barrier_semaphore()
+    near = [up, down] + [{"yh": lax.rem(yh + o, 4)} for o in (1, 2, 3)]
+    for o in range(16):
+        if o:
+            there = lax.rem(state * 2 + c + o, 16)
+            near.append({"yl": there // 8, "x": lax.rem(there // 2, 4), "c": lax.rem(there, 2)})
+    for device in near:
+        pl.semaphore_signal(barrier, inc=1, device_id=device, device_id_type=pl.DeviceIdType.MESH)
+    pl.semaphore_wait(barrier, len(near))
+
     swap = [
         remote(block_ref.at[0], stored.at[pl.ds(0, 4), c], s_send.at[0], s_recv.at[0], sibling),
         remote(site_ref.at[0], stored.at[pl.ds(4, 2), c], s_send.at[1], s_recv.at[1], sibling),
     ]
-    mine.wait()
 
     def pass_up(s, q):
         block = source(q)
@@ -100,18 +112,60 @@
         return remote(rows.at[0, yh], rows.at[0, yh], y_send, y_recv.at[q],
                       {"yh": lax.rem(yh + 4 - TURN[q], 4)})
 
+    def edge_up(s):
+        cut = pl.ds(0, 256 if s == 3 else SITE)
+        return remote(edges.at[slot_up(s), yh, :, cut], edges.at[slot_up(s + 1), yh, :, cut],
+                      e_send, ez_recv.at[0, s + 1], up)
+
+    def edge_down(s):
+        cut = pl.ds(256 if s == 3 else 0, 256 if s == 3 else SITE)
+        return remote(edges.at[slot_down(s), yh, :, cut], edges.at[slot_down(s + 1), yh, :, cut],
+                      e_send, ez_recv.at[1, s + 1], down)
+
+    def edge_side(t, forward, place, lane):
+        here = edges.at[t, place]
+        return remote(here, here, e_send, ey_recv.at[t, lane], ahead if forward else behind)
+
+    def edge_spread(t):
+        edge_side(t, True, yh, 0).start()
+        edge_side(t, False, yh, 1).start()
+
+    def edge_relay(t):
+        edge_side(t, True, yh, 0).wait_recv()
+        edge_side(t, False, yh, 1).wait_recv()
+        if t % 2:
+            edge_side(t, False, lax.rem(yh + 1, 4), 2).start()
+        else:
+            edge_side(t, True, lax.rem(yh + 3, 4), 2).start()
+
+    def edge_hop(s):
+        edge_up(s - 1).wait_recv()
+        edge_down(s - 1).wait_recv()
+        if s < 4:
+            edge_up(s).start()
+            edge_down(s).start()
+            edge_spread(slot_up(s))
+            edge_spread(slot_down(s))
+        else:
+            edge_spread(7)
+
+    own[0].wait()
     pass_up(0, 0).start()
     pass_down(0, 0).start()
     for q in (1, 2, 3):
         give(q).start()
+    own[1].wait()
+    edge_up(0).start()
+    edge_down(0).start()
     for copy in swap:
         copy.start()
-
-    low, high = (current_ref[:, :, 128 * h:128 * (h + 1)].astype(F32).reshape(128, 128) for h in (0, 1))
+    edge_spread(0)
+
+    own[4].wait()
+    low, high = (now[:, :, 128 * h:128 * (h + 1)].astype(F32).reshape(128, 128) for h in (0, 1))
     current = lanes_to_halves(low, high)
-
-    for copy in own:
-        copy.wait()
+    own[2].wait()
+    own[3].wait()
     for copy in swap:
         copy.wait_recv()
     grown[...] = jnp.zeros_like(grown)
@@ -135,17 +189,15 @@
     def along_x(t, other):
         return [moved_copy(t, other, {"x": lax.rem(x + o, 4)}, (4 if other else 0) + o) for o in (1, 2, 3)]
 
-    def multiply(t):
-        left = stored[...].reshape(384, WIDE)
-        right = rows[t, :, :, 0:WIDE].reshape(128, WIDE)
-        product = lax.dot_general(left, right, (((1,), (1,)), ((), ())), preferred_element_type=F32).astype(BF)
-        blocks = product[0:256].reshape(4, 2, 32, 128)
-        for j in (0, 1):
-            proj_out[t, j] = blocks[:, j].reshape(128, 128)
-        moved[t, state] = product[256:384]
+    def send_moved(t):
         moved_copy(t, False, partner, 4).start()
         for copy in along_x(t, False):
             copy.start()
+        if t == 7:
+            for o in (1, 2, 3):
+                moved_copy(t, False, {"yl": 1 - yl, "x": lax.rem(x + o, 4)}, 4 + o).start()
+
+    def send_proj(t):
         home = row_of(t) == state
 
         @pl.when(home)
@@ -157,6 +209,28 @@
             to_state(t, True).start()
 
         to_state(t, False).start()
+
+    def product(t, start, stop):
+        left = stored[start:stop].reshape(64 * (stop - start), WIDE)
+        right = rows[t].reshape(128, WIDE)
+        return lax.dot_general(left, right, (((1,), (1,)), ((), ())), preferred_element_type=F32).astype(BF)
+
+    def keep_proj(t, value):
+        blocks = value.reshape(4, 2, 32, 128)
+        for j in (0, 1):
+            proj_out[t, j] = blocks[:, j].reshape(128, 128)
+
+    def multiply(t):
+        if t == 7:
+            moved[t, state] = product(t, 4, 6)
+            send_moved(t)
+            keep_proj(t, product(t, 0, 4))
+        else:
+            both = product(t, 0, 6)
+            keep_proj(t, both[0:256])
+            moved[t, state] = both[256:384]
+            send_moved(t)
+        send_proj(t)
 
     def relay(t):
         moved_copy(t, False, partner, 4).wait_recv()
@@ -164,11 +238,14 @@
             copy.start()
 
     def grow(t):
+        edge_side(t, t % 2 == 0, yh, 2).wait_recv()
+        if t == 7:
+            moved_copy(t, False, partner, 4).wait_recv()
         for other in (False, True):
             for copy in along_x(t, other):
                 copy.wait_recv()
         for s in (0, 1):
-            site = rows[t, :, :, WIDE + 256 * s:WIDE + 256 * (s + 1)].reshape(128, 256)
+            site = edges[t, :, :, 256 * s:256 * (s + 1)].reshape(128, 256)
             right = moved[t, :, 64 * s:64 * (s + 1), :].reshape(512, 128)
             grown[...] += lax.dot_general(site, right, (((0,), (1,)), ((), ())), preferred_element_type=F32)
 
@@ -192,6 +269,10 @@
                 passing(s - 1, q).wait_recv()
             if (s, q) != (0, 0) and (s < 3 or q in last):
                 passing(s, q).start()
+        if place in HOPS:
+            edge_hop(HOPS[place])
+        for t in RELAYS.get(place, ()):
+            edge_relay(t)
         s, q = UP_ORDER[place]
         if q == 3:
             if s == 0:
@@ -199,13 +280,12 @@
             else:
                 step(slot_up(s))
                 step(slot_down(s))
+    relay(6)
     for q in (0, 1):
         pass_up(3, q).wait_recv()
     for q in (2, 3):
         pass_down(3, q).wait_recv()
     multiply(7)
-    relay(6)
-    relay(7)
     for t in done[-3:]:
         grow(t)
 
@@ -275,12 +355,12 @@
 
     exchange(2, collected(1))
     total = jnp.sum(collected(2), axis=1, keepdims=True) * (1.0 / 4096.0)
-    factor = total * weight_ref[...]
+    factor = [total[k:k + 1] * weight_ref[k] for k in range(8)]
     halves = []
     for i in (0, 1):
         value = current[i]
         for k in range(8):
-            value = value + factor[k:k + 1, :] * proj_in[k, i].astype(F32)
+            value = value + factor[k] * proj_in[k, i].astype(F32)
         halves.append(value)
     low, high = halves_to_lanes(*halves)
     pen_ref[:, :, 0:128] = low.reshape(4, 32, 128)
@@ -301,6 +381,8 @@
         copy.wait_send()
     drained(rows.at[0, pl.ds(0, 3)], y_send)
     drained(rows.at[pl.ds(0, 7)], z_send)
+    drained(edges.at[pl.ds(0, 7)], e_send)
+    drained(edges.at[0, pl.ds(0, 3)], e_send)
     drained(proj_in.at[pl.ds(0, 7)], p_send)
     drained(proj_in.at[0, 0], p_send)
     drained(moved.at[pl.ds(0, 7)], m_send)
@@ -315,8 +397,6 @@
 
 
 def shards(intersect_left, stored_block, stored_site, current_site, current_block, penalty_weight):
-    chunk = jnp.concatenate([intersect_left[0], current_site.reshape(32, SITE)], axis=1)
-    weight = jnp.broadcast_to(penalty_weight[:, None], (8, 128))
     hbm = pl.BlockSpec(memory_space=pl.ANY)
     vmem = pl.BlockSpec(memory_space=pltpu.VMEM)
     dma = pltpu.SemaphoreType.DMA
@@ -326,11 +406,13 @@
             jax.ShapeDtypeStruct((4, 32, 256), F32),
             jax.ShapeDtypeStruct((1, 32, 2048), BF),
         ),
-        in_specs=[hbm, hbm, hbm, vmem, vmem],
+        in_specs=[hbm, hbm, hbm, hbm, hbm, pl.BlockSpec(memory_space=pltpu.SMEM)],
         out_specs=(vmem, vmem),
         scratch_shapes=[
-            pltpu.VMEM((8, 4, 32, COLS), BF),
+            pltpu.VMEM((8, 4, 32, WIDE), BF),
             pltpu.VMEM((6, 2, 32, WIDE), BF),
+            pltpu.VMEM((8, 4, 32, SITE), BF),
+            pltpu.VMEM((4, 32, 256), BF),
             pltpu.VMEM((8, 2, 128, 128), BF),
             pltpu.VMEM((8, 2, 128, 128), BF),
             pltpu.VMEM((8, 8, 128, 128), BF),
@@ -339,12 +421,12 @@
             pltpu.VMEM((8, 4, 16, 128), BF),
             pltpu.VMEM((32, 16, 128), BF),
             pltpu.VMEM((3, 8, 8, 128), F32),
-            dma((3,)), dma, dma((4,)), dma, dma((2, 5, 4)), dma((2,)), dma((2,)), dma, dma((8, 2)),
-            dma, dma((8, 8)), dma, dma, dma, dma, dma((3,)), dma((3,)),
+            dma((5,)), dma, dma((4,)), dma, dma((2, 5, 4)), dma((2,)), dma((2,)), dma, dma((8, 2)),
+            dma, dma((8, 8)), dma, dma, dma, dma, dma((3,)), dma((3,)), dma, dma((2, 5)), dma((8, 3)),
         ],
-        compiler_params=pltpu.CompilerParams(has_side_effects=True, vmem_limit_bytes=48 * 1024 * 1024),
+        compiler_params=pltpu.CompilerParams(collective_id=0, has_side_effects=True, vmem_limit_bytes=63 * 1024 * 1024),
         name="project_and_grow",
-    )(chunk, stored_block, stored_site, current_block, weight)
+    )(intersect_left, stored_block, stored_site, current_site.reshape(32, SITE), current_block, penalty_weight)
 
 
 def solution(mesh):

time: 114 us -> 98.3 us (0.86)
  Pallas kernels: 109 us -> 93.5 us
    pallas_call x1, Pallas kernels: 109 us -> 93.5 us  [shards(): pl.pallas_call(kernel, out_shape=(jax.ShapeDtypeStruct((4, 32, 256), F32)...]
    unnamed x9 -> x5, local copies, waits for them, and re-layouts: 3.12 us -> 3.64 us
where the time goes in v2:
time: 98.3 us; the launch traced here: 97.8 us
  Pallas kernels  93.5 us (95%)
  local copies, waits for them, and re-layouts  3.64 us (4%)
    pallas_call x1, Pallas kernels, shards(): pl.pallas_call(kernel, out_shape=(jax.ShapeDtypeStruct((4, 32, 256), F32)...  93.5 us
    unnamed x5, local copies, waits for them, and re-layouts  3.64 us

profile of v2, /device:TPU:1, one launch (start us, length us, event | category | flops | bytes accessed | tf_op | source)
XLA Modules:
  0.0 97.8 jit_solution(18250976714066286711)
XLA Ops:
  0.6 1.4 %copy.8 = bf16[4,8,2,256]{3,1,2,0:T(8,128)(2,1)} copy(bf16[4,8,2,256]{3,2,1,0:T(2,128)(2,1)} %bitcast.3) | data formatting | bytes 65536
  2.0 93.5 %project_and_grow.1 = (f32[4,32,256]{2,1,0:T(8,128)}, bf16[1,32,2048]{2,1,0:T(8,128)(2,1)}) custom-call(bf16[1,32,2048]{2,1,0:T(8,128)(2,1)} %env_ref.1, bf16[1,4,32,2048]{3,2,1,0:T(8,128)(2,1)} %block_ref.1, bf16[1,2,32,2048]{3,2,1,0:T(8,128)(2,1)} %site_ref.1, bf16[32,512]{1,0:T(8,128)(2,1)} %bitcast.2, bf16[4,32,256]{2,1,0:T(8,128)(2,1)} %current_ref.1, ...), custom_call_target="tpu_custom_call" | custom-call | tf_op jit(solution)/shard_map/project_and_grow/pallas_call | solution.py:403
  95.6 0.0 copy-start
  95.6 1.6 %copy.11 = f32[4,32,256]{2,1,0:T(8,128)} copy(f32[4,32,256]{2,1,0:T(8,128)} %get-tuple-element.4) | data formatting | bytes 262144
  97.2 0.0 copy-done
  97.2 0.7 copy.12
Async XLA Ops:
  95.6 1.6 %copy-start = (bf16[1,32,2048]{2,1,0:T(8,128)(2,1)S(1)}, bf16[1,32,2048]{2,1,0:T(8,128)(2,1)}, u32[]{:S(2)}) copy-start(bf16[1,32,2048]{2,1,0:T(8,128)(2,1)} %get-tuple-element.5) | copy-start | bytes 393220

commit v3 on v1

v3 whole, which is shorter than its diff:
```python
import jax
import jax.numpy as jnp
from jax import lax
from jax.experimental import pallas as pl
from jax.experimental.pallas import tpu as pltpu
from jax.sharding import Mesh
from jax.sharding import PartitionSpec as P

BF = jnp.bfloat16
F32 = jnp.float32
STATE = ("yl", "x")
BOND = ("z", "yh", "c")
WIDE = 2048
SITE = 512

ORDER = [
    (0, 0), (1, 0), (2, 0), (0, 1), (3, 0), (1, 1), (0, 3), (2, 1),
    (0, 2), (1, 3), (3, 1), (1, 2), (2, 3), (2, 2), (3, 3), (3, 2),
]
UNITS = [(0, 0), (1, 0), (2, 0), (3, 0), (1, 1), (2, 1), (3, 1), (4, 0)]
HOPS = {1: 1, 2: 2, 4: 3, 6: 4}
SPREADS = {3: (0,), 5: (1,), 6: (2,), 7: (3,), 9: (4,)}
RELAYS = {8: (0,), 10: (1,), 11: (2,), 13: (3,), 15: (4,)}
TASKS = {
    5: [(0, 1)],
    6: [(0, 0)],
    7: [(0, 2)],
    8: [(1, 1)],
    10: [(0, 3), (1, 0)],
    11: [(0, 4), (1, 2), (2, 1)],
    13: [(0, 5), (1, 3), (2, 0)],
    14: [(2, 2), (1, 4)],
    15: [(0, 6), (3, 1)],
    16: [(1, 5), (2, 3)],
    17: [(3, 0), (3, 2)],
    19: [(2, 4)],
}


def remote(src, dst, send, recv, device):
    return pltpu.make_async_remote_copy(
        src_ref=src, dst_ref=dst, send_sem=send, recv_sem=recv,
        device_id=device, device_id_type=pl.DeviceIdType.MESH,
    )


def lanes_to_halves(low, high):
    lane = lax.broadcasted_iota(jnp.int32, low.shape, 1) // 32
    first = jnp.where(lane == 0, low, jnp.where(lane == 1, pltpu.roll(low, 96, 1),
                      jnp.where(lane == 2, pltpu.roll(high, 64, 1), pltpu.roll(high, 32, 1))))
    second = jnp.where(lane == 0, pltpu.roll(low, 96, 1), jnp.where(lane == 1, pltpu.roll(low, 64, 1),
                       jnp.where(lane == 2, pltpu.roll(high, 32, 1), high)))
    return first, second


def halves_to_lanes(first, second):
    lane = lax.broadcasted_iota(jnp.int32, first.shape, 1) // 32
    low = jnp.where(lane == 0, first, jnp.where(lane == 1, pltpu.roll(second, 32, 1),
                    jnp.where(lane == 2, pltpu.roll(first, 32, 1), pltpu.roll(second, 64, 1))))
    high = jnp.where(lane == 0, pltpu.roll(first, 64, 1), jnp.where(lane == 1, pltpu.roll(second, 96, 1),
                     jnp.where(lane == 2, pltpu.roll(first, 96, 1), second)))
    return low, high


def turned(low, high, blocks):
    lane = lax.broadcasted_iota(jnp.int32, low.shape, 1)
    a, b = pltpu.roll(low, 64, 1), pltpu.roll(high, 64, 1)
    odd = lax.rem(blocks, 2) == 1
    first = jnp.where(odd, jnp.where(lane < 64, a, b), low)
    second = jnp.where(odd, jnp.where(lane < 64, b, a), high)
    swap = blocks >= 2
    return jnp.where(swap, second, first), jnp.where(swap, first, second)


def kernel(env_ref, block_ref, site_ref, edge_ref, current_ref, weight_ref, pen_ref, next_ref,
           rows, stored, edges, now, proj_out, proj_in, moved, grown, grown_in,
           tiles_out, tiles_in, dots, weights, pen_out, next_out,
           local_sem, y_send, y_recv, d_send, d_recv, z_send, z_recv, s_send, s_recv, p_send, p_recv,
           m_send, m_recv, g_send, g_recv, o_send, o_recv, r_send, r_recv, e_send, ed_recv, ez_recv, ey_recv):
    yl, x, z, yh, c = (lax.axis_index(n) for n in ("yl", "x", "z", "yh", "c"))
    state = yl * 4 + x
    onward = {"z": lax.rem(z + 7 + 2 * c, 8)}
    sibling = {"c": 1 - c}
    partner = {"yl": 1 - yl}

    own = [
        pltpu.make_async_copy(env_ref.at[0], rows.at[0, 0, c], local_sem.at[0]),
        pltpu.make_async_copy(edge_ref, edges.at[0, 0, c], local_sem.at[1]),
        pltpu.make_async_copy(block_ref.at[0], stored.at[pl.ds(0, 4), c], local_sem.at[2]),
        pltpu.make_async_copy(site_ref.at[0], stored.at[pl.ds(4, 2), c], local_sem.at[3]),
        pltpu.make_async_copy(current_ref, now, local_sem.at[4]),
        pltpu.make_async_copy(weight_ref, weights, local_sem.at[5]),
    ]
    for copy in own:
        copy.start()

    barrier = pltpu.get_barrier_semaphore()
    near = [{"z": lax.rem(z + 1, 8)}, {"z": lax.rem(z + 7, 8)}] + [{"yh": lax.rem(yh + o, 4)} for o in (1, 2, 3)]
    for o in range(1, 16):
        there = lax.rem(state * 2 + c + o, 16)
        near.append({"yl": there // 8, "x": lax.rem(there // 2, 4), "c": lax.rem(there, 2)})
    for device in near:
        pl.semaphore_signal(barrier, inc=1, device_id=device, device_id_type=pl.DeviceIdType.MESH)
    pl.semaphore_wait(barrier, len(near))

    swap = [
        remote(block_ref.at[0], stored.at[pl.ds(0, 4), c], s_send.at[0], s_recv.at[0], sibling),
        remote(site_ref.at[0], stored.at[pl.ds(4, 2), c], s_send.at[1], s_recv.at[1], sibling),
    ]

    def passing(s, q, other):
        core = 1 - c if other else c
        return remote(rows.at[s, q, core], rows.at[s + 1, q, core], z_send, z_recv.at[s + 1, q, other], onward)

    def give(q):
        return remote(rows.at[0, 0, c], rows.at[0, q, c], y_send, y_recv.at[q], {"yh": lax.rem(yh + 4 - q, 4)})

    def give_far(q):
        half = pl.ds(0 if q == 1 else 16, 16)
        return remote(rows.at[0, q, c, half], rows.at[0, 2, c, half], y_send, y_recv.at[0 if q == 1 else 2],
                      {"yh": lax.rem(yh + 4 - q, 4)})

    def across(q):
        here = rows.at[0, q, c]
        return remote(here, here, d_send, d_recv.at[q], sibling)

    def edge_of(s, place):
        return edges.at[s, place] if s in (1, 2, 3) else edges.at[s, place, c]

    edge_across = remote(edges.at[0, 0, c], edges.at[0, 0, c], e_send, ed_recv, sibling)

    def edge_on(s):
        if s == 3:
            return remote(edges.at[3, 0, c], edges.at[4, 0, c], e_send, ez_recv.at[4], onward)
        return remote(edges.at[s, 0], edges.at[s + 1, 0], e_send, ez_recv.at[s + 1], onward)

    def edge_side(s, q):
        return remote(edge_of(s, 0), edge_of(s, q), e_send, ey_recv.at[s, q], {"yh": lax.rem(yh + 4 - q, 4)})

    def edge_far(s):
        q = 1 + 2 * lax.rem(c + s, 2)
        return remote(edge_of(s, q), edge_of(s, 2), e_send, ey_recv.at[s, 2], {"yh": lax.rem(yh + 4 - q, 4)})

    def edge_spread(s):
        edge_side(s, 1).start()
        edge_side(s, 3).start()

    def edge_relay(s):
        edge_side(s, 1).wait_recv()
        edge_side(s, 3).wait_recv()
        edge_far(s).start()

    def edge_hop(s):
        edge_on(s - 1).wait_recv()
        if s < 4:
            edge_on(s).start()

    own[0].wait()
    passing(0, 0, 0).start()
    across(0).start()
    for q in (1, 3):
        give(q).start()
    own[1].wait()
    edge_across.start()
    across(0).wait_recv()
    passing(0, 0, 1).start()
    edge_across.wait_recv()
    edge_on(0).start()

    own[4].wait()
    special = lax.rem(state + 8 - z, 4) == 0
    low, high = (now[:, :, 128 * h:128 * (h + 1)].astype(F32).reshape(128, 128) for h in (0, 1))
    low, high = turned(low, high, yh)
    current = [jnp.where(special, mixed, plain) for mixed, plain in zip(lanes_to_halves(low, high), (low, high))]
    grown[...] = jnp.zeros_like(grown)

    def origin(u):
        s = UNITS[u][0]
        return lax.rem(z + 8 + s - 2 * s * c, 8)

    def to_state(u, other, at_home=False):
        r = origin(u)
        core = 1 - c if other else c
        s, pair = UNITS[u]
        cut = pl.ds(128 * pair, 128) if s in (1, 2, 3) else pl.ds(pl.multiple_of(128 * c, 128), 128)
        there = proj_in.at[state, :, cut]
        if at_home:
            return pltpu.make_async_copy(proj_out.at[u, core], there, p_recv.at[state])
        return remote(proj_out.at[u, core], there, p_send.at[u, other], p_recv.at[state],
                      {"yl": r // 4, "x": lax.rem(r, 4), "c": core})

    def moved_copy(s, other, device, sem):
        block = moved.at[s, (1 - yl if other else yl) * 4 + x]
        return remote(block, block, m_send, m_recv.at[s, sem], device)

    def along_x(s, other, steps=(1, 2, 3)):
        return [near_x(s, other, o) for o in steps]

    def near_x(s, other, o):
        return moved_copy(s, other, {"x": lax.rem(x + o, 4)}, (4 if other else 0) + o)

    def far_along_x(s, other):
        step = 3 if other else 1
        block = moved.at[s, (1 - yl if other else yl) * 4 + lax.rem(x + 4 - step, 4)]
        return remote(block, block, m_send, m_recv.at[s, (4 if other else 0) + 2], {"x": lax.rem(x + step, 4)})

    def send_moved(s):
        moved_copy(s, False, partner, 4).start()
        for copy in along_x(s, False, (1, 2, 3) if s == 7 else (1, 3)):
            copy.start()

    def send_proj(s):
        home = origin(s) == state

        @pl.when(home)
        def _():
            to_state(s, 0, True).start()

        @pl.when(jnp.logical_not(home))
        def _():
            to_state(s, 0).start()

        to_state(s, 1).start()

    def unit_of(ref, u):
        s, pair = UNITS[u]
        return ref.at[s, pl.ds(2 * pair, 2)] if s in (1, 2, 3) else ref.at[s, :, c]

    def product(u, start, stop):
        left = stored[start:stop].reshape(64 * (stop - start), WIDE)
        right = unit_of(rows, u)[...].reshape(128, WIDE)
        return lax.dot_general(left, right, (((1,), (1,)), ((), ())), preferred_element_type=F32).astype(BF)

    def keep_proj(u, value):
        blocks = value.reshape(4, 2, 32, 128)
        for j in (0, 1):
            proj_out[u, j] = blocks[:, j].reshape(128, 128)

    def multiply(u):
        if u == 7:
            moved[u, state] = product(u, 4, 6)
            send_moved(u)
            keep_proj(u, product(u, 0, 4))
            send_proj(u)
        else:
            both = product(u, 0, 6)
            keep_proj(u, both[0:256])
            moved[u, state] = both[256:384]
            send_moved(u)
            send_proj(u)

    def relay(s):
        moved_copy(s, False, partner, 4).wait_recv()
        for copy in along_x(s, True, (1, 2, 3) if s == 7 else (1, 3)):
            copy.start()

    def relay_far(s):
        near_x(s, False, 1).wait_recv()
        far_along_x(s, False).start()
        near_x(s, True, 3).wait_recv()
        far_along_x(s, True).start()

    seen = set()

    def grow(u):
        s = UNITS[u][0]
        if s not in seen:
            seen.add(s)
            edge_far(s).wait_recv()
        for other, steps in ((False, (2, 3)), (True, (1, 2))):
            for copy in along_x(u, other, (1, 2, 3) if u == 7 else steps):
                copy.wait_recv()
        site = unit_of(edges, u)[...].reshape(128, SITE)
        for p in (0, 1):
            right = moved[u, :, 64 * p:64 * (p + 1), :].reshape(512, 128)
            grown[...] += lax.dot_general(site[:, 256 * p:256 * (p + 1)], right, (((0,), (1,)), ((), ())),
                                          preferred_element_type=F32)

    def tasks(place):
        for task, u in TASKS.get(place, ()):
            (multiply, relay, relay_far, grow)[task](u)

    for place, (s, q) in enumerate(ORDER):
        if (s, q) == (0, 1):
            for near_q in (1, 3):
                give(near_q).wait_recv()
                give_far(near_q).start()
                across(near_q).start()
        if (s, q) == (0, 3):
            for near_q in (1, 3):
                give_far(near_q).wait_recv()
            across(2).start()
        if s == 0 and q:
            passing(0, q, 0).start()
            across(q).wait_recv()
            passing(0, q, 1).start()
        if s:
            passing(s - 1, q, 0).wait_recv()
            passing(s, q, 0).start()
            passing(s - 1, q, 1).wait_recv()
            if s < 3:
                passing(s, q, 1).start()
        if place == 2:
            for copy in swap:
                copy.start()
        if place == 5:
            own[2].wait()
            own[3].wait()
            for copy in swap:
                copy.wait_recv()
        tasks(place)
        if place in HOPS:
            edge_hop(HOPS[place])
        for t in SPREADS.get(place, ()):
            edge_spread(t)
        for t in RELAYS.get(place, ()):
            edge_relay(t)
    for q in (0, 1, 3, 2):
        passing(3, q, 0).wait_recv()
        tasks(16 + q)
    multiply(7)
    relay(6)
    relay_far(5)
    relay(7)
    relay_far(6)
    for u in (3, 4, 5):
        grow(u)

    for k in range(8):
        pltpu.make_async_copy(proj_in.at[k], proj_in.at[k], p_recv.at[k]).wait()

    def projected(k, i):
        return proj_in[k, :, 128 * i:128 * (i + 1)].astype(F32)

    partial = [
        sum(jnp.sum((projected(k, i) * current[i]).reshape(16, 8, 128), axis=0) for i in (0, 1))
        for k in range(8)
    ]
    across_lanes = lax.broadcasted_iota(jnp.int32, (1, 128), 1)
    partial = sum(
        jnp.where(across_lanes == k, jnp.sum(jnp.sum(p, axis=0, keepdims=True), axis=1, keepdims=True), 0.0)
        for k, p in enumerate(partial)
    )

    places = (state * 2 + c, z * 4 + yh)
    sizes = (16, 32)

    def peer(stage, o):
        there = lax.rem(places[stage] + o, sizes[stage])
        if stage == 0:
            return {"yl": there // 8, "x": lax.rem(there // 2, 4), "c": lax.rem(there, 2)}
        return {"z": there // 4, "yh": lax.rem(there, 4)}

    def exchange(stage, value):
        dots[stage, places[stage]] = value
        for o in range(1, sizes[stage]):
            here = dots.at[stage, places[stage]]
            remote(here, here, r_send.at[stage], r_recv.at[stage], peer(stage, o)).start()

    def collected(stage):
        others = dots.at[stage, pl.ds(0, sizes[stage] - 1)]
        pltpu.make_async_copy(others, others, r_recv.at[stage]).wait()
        return jnp.sum(dots[stage, 0:sizes[stage]], axis=0)

    exchange(0, partial)
    grow(6)
    grow(7)
    give_half = remote(grown.at[pl.ds(128 * (1 - c), 128)], grown_in, g_send, g_recv, sibling)
    give_half.start()
    give_half.wait_recv()

    lane = lax.broadcasted_iota(jnp.int32, (16, 128), 1)
    half = grown.at[pl.ds(pl.multiple_of(128 * c, 128), 128)]
    for d in range(4):
        for pair in range(4):
            cut = pl.ds(128 * pair, 128)
            first = half[pl.ds(32 * d, 16), cut] + grown_in[pl.ds(32 * d, 16), cut]
            second = half[pl.ds(32 * d + 16, 16), cut] + grown_in[pl.ds(32 * d + 16, 16), cut]
            tiles_out[2 * pair, d] = jnp.where(lane < 64, first, pltpu.roll(second, 64, 1)).astype(BF)
            tiles_out[2 * pair + 1, d] = jnp.where(lane < 64, pltpu.roll(first, 64, 1), second).astype(BF)

    place = z * 4 + yh
    for k in range(8):
        for d in range(4):
            to = 2 * c + d // 2
            here = jnp.logical_and(jnp.logical_and(k == state, z == state), jnp.logical_and(to == yh, d % 2 == c))

            @pl.when(here)
            def _():
                pltpu.make_async_copy(tiles_out.at[k, d], tiles_in.at[place], o_recv).start()

            @pl.when(jnp.logical_not(here))
            def _():
                remote(tiles_out.at[k, d], tiles_in.at[place], o_send, o_recv,
                       {"yl": k // 4, "x": k % 4, "z": state, "yh": to, "c": d % 2}).start()

    exchange(1, collected(0))
    own[5].wait()
    total = collected(1) * (1.0 / 4096.0)
    factor = [total[:, k:k + 1] * weights[k] for k in range(8)]
    halves = []
    for i in (0, 1):
        value = current[i]
        for k in range(8):
            value = value + factor[k] * projected(k, i)
        halves.append(value)
    low, high = (jnp.where(special, mixed, plain) for mixed, plain in zip(halves_to_lanes(*halves), halves))
    low, high = turned(low, high, lax.rem(4 - yh, 4))
    pen_out[:, :, 0:128] = low.reshape(4, 32, 128)
    pen_out[:, :, 128:256] = high.reshape(4, 32, 128)

    pen_copy = pltpu.make_async_copy(pen_out, pen_ref, local_sem.at[1])
    pen_copy.start()

    pltpu.make_async_copy(tiles_in, tiles_in, o_recv).wait()
    for p in range(16):
        even = tiles_in[2 * p].astype(F32)
        odd = tiles_in[2 * p + 1].astype(F32)
        cut = slice(128 * p, 128 * (p + 1))
        next_out[ 0:16, cut] = jnp.where(lane < 64, even, pltpu.roll(odd, 64, 1)).astype(BF)
        next_out[ 16:32, cut] = jnp.where(lane < 64, pltpu.roll(even, 64, 1), odd).astype(BF)

    next_copy = pltpu.make_async_copy(next_out, next_ref.at[0], local_sem.at[0])
    next_copy.start()

    def drained(ref, sem):
        pltpu.make_async_copy(ref, ref, sem).wait()

    for copy in swap:
        copy.wait_send()
    drained(rows.at[0, pl.ds(0, 3), 0], y_send)
    drained(rows.at[0, :, 0], d_send)
    drained(rows.at[pl.ds(0, 3)], z_send)
    drained(rows.at[3, :, 0], z_send)
    drained(edges.at[pl.ds(0, 4)], e_send)
    for t in range(8):
        @pl.when(origin(t) != state)
        def _():
            to_state(t, 0).wait_send()

        to_state(t, 1).wait_send()
    drained(moved.at[pl.ds(0, 7)], m_send)
    give_half.wait_send()
    for stage in range(2):
        drained(dots.at[stage, pl.ds(0, sizes[stage] - 1)], r_send.at[stage])
    drained(tiles_in.at[pl.ds(0, 31)], o_send)

    @pl.when(jnp.logical_not(jnp.logical_and(z == state, yh // 2 == c)))
    def _():
        drained(tiles_in.at[0], o_send)
    next_copy.wait()
    pen_copy.wait()


def shards(intersect_left, stored_block, stored_site, current_site, current_block, penalty_weight):
    hbm = pl.BlockSpec(memory_space=pl.ANY)
    dma = pltpu.SemaphoreType.DMA
    return pl.pallas_call(
        kernel,
        out_shape=(
            jax.ShapeDtypeStruct((4, 32, 256), F32),
            jax.ShapeDtypeStruct((1, 32, 2048), BF),
        ),
        in_specs=[hbm] * 6,
        out_specs=(hbm, hbm),
        scratch_shapes=[
            pltpu.VMEM((5, 4, 2, 32, WIDE), BF),
            pltpu.VMEM((6, 2, 32, WIDE), BF),
            pltpu.VMEM((5, 4, 2, 32, SITE), BF),
            pltpu.VMEM((4, 32, 256), BF),
            pltpu.VMEM((8, 2, 128, 128), BF),
            pltpu.VMEM((8, 128, 256), BF),
            pltpu.VMEM((8, 8, 128, 128), BF),
            pltpu.VMEM((256, 512), F32),
            pltpu.VMEM((128, 512), F32),
            pltpu.VMEM((8, 4, 16, 128), BF),
            pltpu.VMEM((32, 16, 128), BF),
            pltpu.VMEM((2, 32, 1, 128), F32),
            pltpu.SMEM((8,), F32),
            pltpu.VMEM((4, 32, 256), F32),
            pltpu.VMEM((32, 2048), BF),
            dma((6,)), dma, dma((4,)), dma, dma((4,)), dma, dma((5, 4, 2)), dma((2,)), dma((2,)), dma((8, 2)), dma((8,)),
            dma, dma((8, 8)), dma, dma, dma, dma, dma((2,)), dma((2,)), dma, dma, dma((5,)), dma((5, 4)),
        ],
        compiler_params=pltpu.CompilerParams(collective_id=0, has_side_effects=True, vmem_limit_bytes=63 * 1024 * 1024),
        name="project_and_grow",
    )(intersect_left, stored_block, stored_site, current_site.reshape(32, SITE), current_block, penalty_weight)


def solution(mesh):
    torus = Mesh(mesh.devices.reshape(2, 4, 8, 4, 2), STATE + BOND)
    in_specs = (
        P(STATE, BOND, None),
        P(STATE, None, BOND, None),
        P(STATE, None, BOND, None),
        P(BOND, None, STATE),
        P(None, BOND, STATE),
        P(),
    )
    out_specs = (P(None, BOND, STATE), P(STATE, BOND, None))
    return jax.shard_map(shards, mesh=torus, in_specs=in_specs, out_specs=out_specs, check_vma=False)
```

time: 114 us -> 91.7 us (0.80)
  Pallas kernels: 109 us -> 87.2 us
    pallas_call x1, Pallas kernels: 109 us -> 87.2 us  [shards(): pl.pallas_call(kernel, out_shape=(jax.ShapeDtypeStruct((4, 32, 256), F32)...]
    unnamed x9 -> x5, local copies, waits for them, and re-layouts: 3.12 us -> 3.64 us
where the time goes in v3:
time: 91.7 us; the launch traced here: 91.5 us
  Pallas kernels  87.2 us (95%)
  local copies, waits for them, and re-layouts  3.64 us (4%)
    pallas_call x1, Pallas kernels, shards(): pl.pallas_call(kernel, out_shape=(jax.ShapeDtypeStruct((4, 32, 256), F32)...  87.2 us
    unnamed x5, local copies, waits for them, and re-layouts  3.64 us

profile of v3, /device:TPU:1, one launch (start us, length us, event | category | flops | bytes accessed | tf_op | source)
XLA Modules:
  0.0 91.5 jit_solution(1924279302156286820)
XLA Ops:
  0.6 1.4 %copy.8 = bf16[4,8,2,256]{3,1,2,0:T(8,128)(2,1)} copy(bf16[4,8,2,256]{3,2,1,0:T(2,128)(2,1)} %bitcast.3) | data formatting | bytes 65536
  2.0 87.2 %project_and_grow.1 = (f32[4,32,256]{2,1,0:T(8,128)}, bf16[1,32,2048]{2,1,0:T(8,128)(2,1)}) custom-call(bf16[1,32,2048]{2,1,0:T(8,128)(2,1)} %env_ref.1, bf16[1,4,32,2048]{3,2,1,0:T(8,128)(2,1)} %block_ref.1, bf16[1,2,32,2048]{3,2,1,0:T(8,128)(2,1)} %site_ref.1, bf16[32,512]{1,0:T(8,128)(2,1)} %bitcast.2, bf16[4,32,256]{2,1,0:T(8,128)(2,1)} %current_ref.1, ...), custom_call_target="tpu_custom_call" | custom-call | tf_op jit(solution)/shard_map/project_and_grow/pallas_call | solution.py:458
  89.2 0.0 copy-start
  89.2 1.6 %copy.11 = f32[4,32,256]{2,1,0:T(8,128)} copy(f32[4,32,256]{2,1,0:T(8,128)} %get-tuple-element.4) | data formatting | bytes 262144
  90.8 0.0 copy-done
  90.8 0.7 copy.12
Async XLA Ops:
  89.2 1.6 %copy-start = (bf16[1,32,2048]{2,1,0:T(8,128)(2,1)S(1)}, bf16[1,32,2048]{2,1,0:T(8,128)(2,1)}, u32[]{:S(2)}) copy-start(bf16[1,32,2048]{2,1,0:T(8,128)(2,1)} %get-tuple-element.5) | copy-start | bytes 393220

commit v4 on v3

--- a/solution.py
+++ b/solution.py
@@ -19,15 +19,14 @@
 ]
 UNITS = [(0, 0), (1, 0), (2, 0), (3, 0), (1, 1), (2, 1), (3, 1), (4, 0)]
 HOPS = {1: 1, 2: 2, 4: 3, 6: 4}
-SPREADS = {3: (0,), 5: (1,), 6: (2,), 7: (3,), 9: (4,)}
-RELAYS = {8: (0,), 10: (1,), 11: (2,), 13: (3,), 15: (4,)}
+SPREADS = {3: (0,), 5: (1,), 7: (2,), 10: (3,), 12: (4,)}
+RELAYS = {9: (0,), 11: (1,), 12: (2,), 14: (3,), 15: (4,)}
 TASKS = {
     5: [(0, 1)],
-    6: [(0, 0)],
     7: [(0, 2)],
-    8: [(1, 1)],
-    10: [(0, 3), (1, 0)],
-    11: [(0, 4), (1, 2), (2, 1)],
+    8: [(0, 0), (1, 1)],
+    10: [(0, 3)],
+    11: [(0, 4), (1, 0), (1, 2), (2, 1)],
     13: [(0, 5), (1, 3), (2, 0)],
     14: [(2, 2), (1, 4)],
     15: [(0, 6), (3, 1)],
@@ -42,24 +41,6 @@
         src_ref=src, dst_ref=dst, send_sem=send, recv_sem=recv,
         device_id=device, device_id_type=pl.DeviceIdType.MESH,
     )
-
-
-def lanes_to_halves(low, high):
-    lane = lax.broadcasted_iota(jnp.int32, low.shape, 1) // 32
-    first = jnp.where(lane == 0, low, jnp.where(lane == 1, pltpu.roll(low, 96, 1),
-                      jnp.where(lane == 2, pltpu.roll(high, 64, 1), pltpu.roll(high, 32, 1))))
-    second = jnp.where(lane == 0, pltpu.roll(low, 96, 1), jnp.where(lane == 1, pltpu.roll(low, 64, 1),
-                       jnp.where(lane == 2, pltpu.roll(high, 32, 1), high)))
-    return first, second
-
-
-def halves_to_lanes(first, second):
-    lane = lax.broadcasted_iota(jnp.int32, first.shape, 1) // 32
-    low = jnp.where(lane == 0, first, jnp.where(lane == 1, pltpu.roll(second, 32, 1),
-                    jnp.where(lane == 2, pltpu.roll(first, 32, 1), pltpu.roll(second, 64, 1))))
-    high = jnp.where(lane == 0, pltpu.roll(first, 64, 1), jnp.where(lane == 1, pltpu.roll(second, 96, 1),
-                     jnp.where(lane == 2, pltpu.roll(first, 96, 1), second)))
-    return low, high
 
 
 def turned(low, high, blocks):
@@ -74,9 +55,9 @@
 
 def kernel(env_ref, block_ref, site_ref, edge_ref, current_ref, weight_ref, pen_ref, next_ref,
            rows, stored, edges, now, proj_out, proj_in, moved, grown, grown_in,
-           tiles_out, tiles_in, dots, weights, pen_out, next_out,
-           local_sem, y_send, y_recv, d_send, d_recv, z_send, z_recv, s_send, s_recv, p_send, p_recv,
-           m_send, m_recv, g_send, g_recv, o_send, o_recv, r_send, r_recv, e_send, ed_recv, ez_recv, ey_recv):
+           tiles_out, tiles_in, dots, weights, pen_out, next_out, pairs,
+           local_sem, sent, y_recv, d_recv, z_recv, s_recv, p_recv, m_recv, g_recv, o_recv, r_recv,
+           ed_recv, ez_recv, ey_recv):
     yl, x, z, yh, c = (lax.axis_index(n) for n in ("yl", "x", "z", "yh", "c"))
     state = yl * 4 + x
     onward = {"z": lax.rem(z + 7 + 2 * c, 8)}
@@ -85,7 +66,7 @@
 
     own = [
         pltpu.make_async_copy(env_ref.at[0], rows.at[0, 0, c], local_sem.at[0]),
-        pltpu.make_async_copy(edge_ref, edges.at[0, 0, c], local_sem.at[1]),
+        pltpu.make_async_copy(edge_ref, pairs, local_sem.at[1]),
         pltpu.make_async_copy(block_ref.at[0], stored.at[pl.ds(0, 4), c], local_sem.at[2]),
         pltpu.make_async_copy(site_ref.at[0], stored.at[pl.ds(4, 2), c], local_sem.at[3]),
         pltpu.make_async_copy(current_ref, now, local_sem.at[4]),
@@ -101,54 +82,78 @@
         near.append({"yl": there // 8, "x": lax.rem(there // 2, 4), "c": lax.rem(there, 2)})
     for device in near:
         pl.semaphore_signal(barrier, inc=1, device_id=device, device_id_type=pl.DeviceIdType.MESH)
+    own[1].wait()
+    for p in (0, 1):
+        edges[0, 0, c, :, 256 * p:256 * (p + 1)] = pairs[:, p, :]
     pl.semaphore_wait(barrier, len(near))
 
     swap = [
-        remote(block_ref.at[0], stored.at[pl.ds(0, 4), c], s_send.at[0], s_recv.at[0], sibling),
-        remote(site_ref.at[0], stored.at[pl.ds(4, 2), c], s_send.at[1], s_recv.at[1], sibling),
+        remote(block_ref.at[0], stored.at[pl.ds(0, 4), c], sent, s_recv, sibling),
+        remote(site_ref.at[0], stored.at[pl.ds(4, 2), c], sent, s_recv, sibling),
     ]
 
     def passing(s, q, other):
         core = 1 - c if other else c
-        return remote(rows.at[s, q, core], rows.at[s + 1, q, core], z_send, z_recv.at[s + 1, q, other], onward)
+        return remote(rows.at[s, q, core], rows.at[s + 1, q, core], sent, z_recv.at[s, q, other], onward)
 
     def give(q):
-        return remote(rows.at[0, 0, c], rows.at[0, q, c], y_send, y_recv.at[q], {"yh": lax.rem(yh + 4 - q, 4)})
+        return remote(rows.at[0, 0, c], rows.at[0, q, c], sent, y_recv.at[q], {"yh": lax.rem(yh + 4 - q, 4)})
 
     def give_far(q):
         half = pl.ds(0 if q == 1 else 16, 16)
-        return remote(rows.at[0, q, c, half], rows.at[0, 2, c, half], y_send, y_recv.at[0 if q == 1 else 2],
+        return remote(rows.at[0, q, c, half], rows.at[0, 2, c, half], sent, y_recv.at[0 if q == 1 else 2],
                       {"yh": lax.rem(yh + 4 - q, 4)})
 
     def across(q):
         here = rows.at[0, q, c]
-        return remote(here, here, d_send, d_recv.at[q], sibling)
+        return remote(here, here, sent, d_recv.at[q], sibling)
 
     def edge_of(s, place):
-        return edges.at[s, place] if s in (1, 2, 3) else edges.at[s, place, c]
-
-    edge_across = remote(edges.at[0, 0, c], edges.at[0, 0, c], e_send, ed_recv, sibling)
+        return edges.at[s, place]
+
+    edge_across = remote(edges.at[0, 0, c], edges.at[0, 0, c], sent, ed_recv, sibling)
 
     def edge_on(s):
-        if s == 3:
-            return remote(edges.at[3, 0, c], edges.at[4, 0, c], e_send, ez_recv.at[4], onward)
-        return remote(edges.at[s, 0], edges.at[s + 1, 0], e_send, ez_recv.at[s + 1], onward)
+        return remote(edges.at[s, 0], edges.at[s + 1, 0], sent, ez_recv.at[s], onward)
 
     def edge_side(s, q):
-        return remote(edge_of(s, 0), edge_of(s, q), e_send, ey_recv.at[s, q], {"yh": lax.rem(yh + 4 - q, 4)})
+        return remote(edge_of(s, 0), edge_of(s, q), sent, ey_recv.at[s, 0], {"yh": lax.rem(yh + 4 - q, 4)})
 
     def edge_far(s):
-        q = 1 + 2 * lax.rem(c + s, 2)
-        return remote(edge_of(s, q), edge_of(s, 2), e_send, ey_recv.at[s, 2], {"yh": lax.rem(yh + 4 - q, 4)})
+        q = 1 + 2 * lax.rem(c + s, 2) if s in (1, 2, 3) else 3
+        return remote(edge_of(s, q), edge_of(s, 2), sent, ey_recv.at[s, 1], {"yh": lax.rem(yh + 4 - q, 4)})
 
     def edge_spread(s):
-        edge_side(s, 1).start()
-        edge_side(s, 3).start()
+        def side(q, core):
+            @pl.when(jnp.logical_or(s in (1, 2, 3), c == core))
+            def _():
+                edge_side(s, q).start()
+
+        side(1, 1)
+        side(3, 0)
 
     def edge_relay(s):
-        edge_side(s, 1).wait_recv()
-        edge_side(s, 3).wait_recv()
-        edge_far(s).start()
+        if s in (1, 2, 3):
+            both = edges.at[s, pl.ds(0, 2)]
+            pltpu.make_async_copy(both, both, ey_recv.at[s, 0]).wait()
+            edge_far(s).start()
+        else:
+            @pl.when(c == 0)
+            def _():
+                edge_side(s, 3).wait_recv()
+                edge_far(s).start()
+
+    def edge_last(s):
+        if s in (1, 2, 3):
+            edge_far(s).wait_recv()
+        else:
+            @pl.when(c == 1)
+            def _():
+                edge_side(s, 1).wait_recv()
+
+            @pl.when(c == 0)
+            def _():
+                edge_far(s).wait_recv()
 
     def edge_hop(s):
         edge_on(s - 1).wait_recv()
@@ -160,7 +165,6 @@
     across(0).start()
     for q in (1, 3):
         give(q).start()
-    own[1].wait()
     edge_across.start()
     across(0).wait_recv()
     passing(0, 0, 1).start()
@@ -168,10 +172,8 @@
     edge_on(0).start()
 
     own[4].wait()
-    special = lax.rem(state + 8 - z, 4) == 0
     low, high = (now[:, :, 128 * h:128 * (h + 1)].astype(F32).reshape(128, 128) for h in (0, 1))
-    low, high = turned(low, high, yh)
-    current = [jnp.where(special, mixed, plain) for mixed, plain in zip(lanes_to_halves(low, high), (low, high))]
+    current = turned(low, high, yh)
     grown[...] = jnp.zeros_like(grown)
 
     def origin(u):
@@ -182,30 +184,30 @@
         r = origin(u)
         core = 1 - c if other else c
         s, pair = UNITS[u]
-        cut = pl.ds(128 * pair, 128) if s in (1, 2, 3) else pl.ds(pl.multiple_of(128 * c, 128), 128)
+        cut = pl.ds(128 * pair, 128) if s in (1, 2, 3) else pl.ds(pl.multiple_of(128 * (1 - c), 128), 128)
         there = proj_in.at[state, :, cut]
         if at_home:
-            return pltpu.make_async_copy(proj_out.at[u, core], there, p_recv.at[state])
-        return remote(proj_out.at[u, core], there, p_send.at[u, other], p_recv.at[state],
+            return pltpu.make_async_copy(proj_out.at[u, core], there, p_recv)
+        return remote(proj_out.at[u, core], there, sent, p_recv,
                       {"yl": r // 4, "x": lax.rem(r, 4), "c": core})
 
     def moved_copy(s, other, device, sem):
         block = moved.at[s, (1 - yl if other else yl) * 4 + x]
-        return remote(block, block, m_send, m_recv.at[s, sem], device)
+        return remote(block, block, sent, m_recv.at[s, sem], device)
 
     def along_x(s, other, steps=(1, 2, 3)):
         return [near_x(s, other, o) for o in steps]
 
     def near_x(s, other, o):
-        return moved_copy(s, other, {"x": lax.rem(x + o, 4)}, (4 if other else 0) + o)
+        return moved_copy(s, other, {"x": lax.rem(x + o, 4)}, 1 if o == (3 if other else 1) else 2)
 
     def far_along_x(s, other):
         step = 3 if other else 1
         block = moved.at[s, (1 - yl if other else yl) * 4 + lax.rem(x + 4 - step, 4)]
-        return remote(block, block, m_send, m_recv.at[s, (4 if other else 0) + 2], {"x": lax.rem(x + step, 4)})
+        return remote(block, block, sent, m_recv.at[s, 2], {"x": lax.rem(x + step, 4)})
 
     def send_moved(s):
-        moved_copy(s, False, partner, 4).start()
+        moved_copy(s, False, partner, 0).start()
         for copy in along_x(s, False, (1, 2, 3) if s == 7 else (1, 3)):
             copy.start()
 
@@ -224,7 +226,7 @@
 
     def unit_of(ref, u):
         s, pair = UNITS[u]
-        return ref.at[s, pl.ds(2 * pair, 2)] if s in (1, 2, 3) else ref.at[s, :, c]
+        return ref.at[s, pl.ds(2 * pair if s in (1, 2, 3) else 2 * (1 - c), 2)]
 
     def product(u, start, stop):
         left = stored[start:stop].reshape(64 * (stop - start), WIDE)
@@ -249,15 +251,18 @@
             send_moved(u)
             send_proj(u)
 
+    def moved_here(s, count, sem):
+        blocks = moved.at[s, pl.ds(0, count)]
+        pltpu.make_async_copy(blocks, blocks, m_recv.at[s, sem]).wait()
+
     def relay(s):
-        moved_copy(s, False, partner, 4).wait_recv()
+        moved_copy(s, False, partner, 0).wait_recv()
         for copy in along_x(s, True, (1, 2, 3) if s == 7 else (1, 3)):
             copy.start()
 
     def relay_far(s):
-        near_x(s, False, 1).wait_recv()
+        moved_here(s, 2, 1)
         far_along_x(s, False).start()
-        near_x(s, True, 3).wait_recv()
         far_along_x(s, True).start()
 
     seen = set()
@@ -266,10 +271,10 @@
         s = UNITS[u][0]
         if s not in seen:
             seen.add(s)
-            edge_far(s).wait_recv()
-        for other, steps in ((False, (2, 3)), (True, (1, 2))):
-            for copy in along_x(u, other, (1, 2, 3) if u == 7 else steps):
-                copy.wait_recv()
+            edge_last(s)
+        if u == 7:
+            moved_here(u, 2, 1)
+        moved_here(u, 4, 2)
         site = unit_of(edges, u)[...].reshape(128, SITE)
         for p in (0, 1):
             right = moved[u, :, 64 * p:64 * (p + 1), :].reshape(512, 128)
@@ -279,6 +284,18 @@
     def tasks(place):
         for task, u in TASKS.get(place, ()):
             (multiply, relay, relay_far, grow)[task](u)
+
+    def last_chunks(core, chunks):
+        @pl.when(c == core)
+        def _():
+            for q in chunks:
+                for other in (0, 1):
+                    passing(3, q, other).wait_recv()
+
+    def last_row(core):
+        @pl.when(c == core)
+        def _():
+            multiply(7)
 
     for place, (s, q) in enumerate(ORDER):
         if (s, q) == (0, 1):
@@ -295,39 +312,51 @@
             across(q).wait_recv()
             passing(0, q, 1).start()
         if s:
-            passing(s - 1, q, 0).wait_recv()
-            passing(s, q, 0).start()
-            passing(s - 1, q, 1).wait_recv()
-            if s < 3:
-                passing(s, q, 1).start()
+            for other in (0, 1):
+                passing(s - 1, q, other).wait_recv()
+
+                @pl.when(jnp.logical_or(s < 3, c == (1 if q < 2 else 0)))
+                def _():
+                    passing(s, q, other).start()
         if place == 2:
             for copy in swap:
                 copy.start()
         if place == 5:
             own[2].wait()
             own[3].wait()
-            for copy in swap:
-                copy.wait_recv()
+            pltpu.make_async_copy(stored.at[:, c], stored.at[:, c], s_recv).wait()
+        if place == 13:
+            last_chunks(1, (0, 1))
+            last_row(1)
         tasks(place)
+        if place == 15:
+            @pl.when(c == 1)
+            def _():
+                relay(7)
         if place in HOPS:
             edge_hop(HOPS[place])
         for t in SPREADS.get(place, ()):
             edge_spread(t)
         for t in RELAYS.get(place, ()):
             edge_relay(t)
-    for q in (0, 1, 3, 2):
-        passing(3, q, 0).wait_recv()
-        tasks(16 + q)
-    multiply(7)
+    tasks(16)
+    last_chunks(0, (3,))
     relay(6)
+    tasks(17)
+    last_chunks(0, (2,))
+    last_row(0)
     relay_far(5)
-    relay(7)
+    tasks(19)
+
+    @pl.when(c == 0)
+    def _():
+        relay(7)
+
     relay_far(6)
     for u in (3, 4, 5):
         grow(u)
 
-    for k in range(8):
-        pltpu.make_async_copy(proj_in.at[k], proj_in.at[k], p_recv.at[k]).wait()
+    pltpu.make_async_copy(proj_in, proj_in, p_recv).wait()
 
     def projected(k, i):
         return proj_in[k, :, 128 * i:128 * (i + 1)].astype(F32)
@@ -355,7 +384,7 @@
         dots[stage, places[stage]] = value
         for o in range(1, sizes[stage]):
             here = dots.at[stage, places[stage]]
-            remote(here, here, r_send.at[stage], r_recv.at[stage], peer(stage, o)).start()
+            remote(here, here, sent, r_recv.at[stage], peer(stage, o)).start()
 
     def collected(stage):
         others = dots.at[stage, pl.ds(0, sizes[stage] - 1)]
@@ -365,7 +394,7 @@
     exchange(0, partial)
     grow(6)
     grow(7)
-    give_half = remote(grown.at[pl.ds(128 * (1 - c), 128)], grown_in, g_send, g_recv, sibling)
+    give_half = remote(grown.at[pl.ds(128 * (1 - c), 128)], grown_in, sent, g_recv, sibling)
     give_half.start()
     give_half.wait_recv()
 
@@ -391,7 +420,7 @@
 
             @pl.when(jnp.logical_not(here))
             def _():
-                remote(tiles_out.at[k, d], tiles_in.at[place], o_send, o_recv,
+                remote(tiles_out.at[k, d], tiles_in.at[place], sent, o_recv,
                        {"yl": k // 4, "x": k % 4, "z": state, "yh": to, "c": d % 2}).start()
 
     exchange(1, collected(0))
@@ -404,8 +433,7 @@
         for k in range(8):
             value = value + factor[k] * projected(k, i)
         halves.append(value)
-    low, high = (jnp.where(special, mixed, plain) for mixed, plain in zip(halves_to_lanes(*halves), halves))
-    low, high = turned(low, high, lax.rem(4 - yh, 4))
+    low, high = turned(*halves, lax.rem(4 - yh, 4))
     pen_out[:, :, 0:128] = low.reshape(4, 32, 128)
     pen_out[:, :, 128:256] = high.reshape(4, 32, 128)
 
@@ -426,28 +454,34 @@
     def drained(ref, sem):
         pltpu.make_async_copy(ref, ref, sem).wait()
 
-    for copy in swap:
-        copy.wait_send()
-    drained(rows.at[0, pl.ds(0, 3), 0], y_send)
-    drained(rows.at[0, :, 0], d_send)
-    drained(rows.at[pl.ds(0, 3)], z_send)
-    drained(rows.at[3, :, 0], z_send)
-    drained(edges.at[pl.ds(0, 4)], e_send)
+    drained(stored.at[:, c], sent)
+    drained(rows.at[0, pl.ds(0, 3), 0], sent)
+    drained(rows.at[0, :, 0], sent)
+    drained(rows.at[pl.ds(0, 3)], sent)
+    drained(rows.at[3, :, 0], sent)
+    drained(edges.at[pl.ds(0, 3)], sent)
+    drained(edges.at[3, pl.ds(0, 3)], sent)
+    drained(edges.at[3, 3, 0], sent)
+
+    @pl.when(c == 0)
+    def _():
+        drained(edges.at[0, pl.ds(0, 2)], sent)
+
     for t in range(8):
         @pl.when(origin(t) != state)
         def _():
-            to_state(t, 0).wait_send()
-
-        to_state(t, 1).wait_send()
-    drained(moved.at[pl.ds(0, 7)], m_send)
-    give_half.wait_send()
+            drained(proj_out.at[0, 0], sent)
+
+    drained(proj_out.at[pl.ds(0, 4)], sent)
+    drained(moved.at[pl.ds(0, 7)], sent)
+    drained(grown_in, sent)
     for stage in range(2):
-        drained(dots.at[stage, pl.ds(0, sizes[stage] - 1)], r_send.at[stage])
-    drained(tiles_in.at[pl.ds(0, 31)], o_send)
+        drained(dots.at[stage, pl.ds(0, sizes[stage] - 1)], sent)
+    drained(tiles_in.at[pl.ds(0, 31)], sent)
 
     @pl.when(jnp.logical_not(jnp.logical_and(z == state, yh // 2 == c)))
     def _():
-        drained(tiles_in.at[0], o_send)
+        drained(tiles_in.at[0], sent)
     next_copy.wait()
     pen_copy.wait()
 
@@ -479,12 +513,13 @@
             pltpu.SMEM((8,), F32),
             pltpu.VMEM((4, 32, 256), F32),
             pltpu.VMEM((32, 2048), BF),
-            dma((6,)), dma, dma((4,)), dma, dma((4,)), dma, dma((5, 4, 2)), dma((2,)), dma((2,)), dma((8, 2)), dma((8,)),
-            dma, dma((8, 8)), dma, dma, dma, dma, dma((2,)), dma((2,)), dma, dma, dma((5,)), dma((5, 4)),
+            pltpu.VMEM((32, 2, 256), BF),
+            dma((6,)), dma, dma((4,)), dma((4,)), dma((4, 4, 2)), dma, dma, dma((8, 3)), dma, dma, dma((2,)),
+            dma, dma((4,)), dma((5, 2)),
         ],
         compiler_params=pltpu.CompilerParams(collective_id=0, has_side_effects=True, vmem_limit_bytes=63 * 1024 * 1024),
         name="project_and_grow",
-    )(intersect_left, stored_block, stored_site, current_site.reshape(32, SITE), current_block, penalty_weight)
+    )(intersect_left, stored_block, stored_site, current_site, current_block, penalty_weight)
 
 
 def solution(mesh):

time: 91.7 us -> 87.2 us (0.951)
  Pallas kernels: 87.2 us -> 84.1 us
  local copies, waits for them, and re-layouts: 3.64 us -> 2.26 us
    pallas_call x1, Pallas kernels: 87.2 us -> 84.1 us  [shards(): pl.pallas_call(kernel, out_shape=(jax.ShapeDtypeStruct((4, 32, 256), F32)...]
    unnamed x5 -> x4, local copies, waits for them, and re-layouts: 3.64 us -> 2.26 us
where the time goes in v4:
time: 87.2 us; the launch traced here: 87 us
  Pallas kernels  84.1 us (96%)
  local copies, waits for them, and re-layouts  2.26 us (3%)
    pallas_call x1, Pallas kernels, shards(): pl.pallas_call(kernel, out_shape=(jax.ShapeDtypeStruct((4, 32, 256), F32)...  84.1 us
    unnamed x4, local copies, waits for them, and re-layouts  2.26 us

profile of v4, /device:TPU:1, one launch (start us, length us, event | category | flops | bytes accessed | tf_op | source)
XLA Modules:
  0.0 87.0 jit_solution(9026950939141081925)
XLA Ops:
  0.6 84.1 %project_and_grow.1 = (f32[4,32,256]{2,1,0:T(8,128)}, bf16[1,32,2048]{2,1,0:T(8,128)(2,1)}) custom-call(bf16[1,32,2048]{2,1,0:T(8,128)(2,1)} %env_ref.1, bf16[1,4,32,2048]{3,2,1,0:T(8,128)(2,1)} %block_ref.1, bf16[1,2,32,2048]{3,2,1,0:T(8,128)(2,1)} %site_ref.1, bf16[32,2,256]{2,1,0:T(2,128)(2,1)} %edge_ref.1, bf16[4,32,256]{2,1,0:T(8,128)(2,1)} %current_ref.1, ...), custom_call_target="tpu_custom_call" | custom-call | tf_op jit(solution)/shard_map/project_and_grow/pallas_call | solution.py:492
  84.8 0.0 copy-start
  84.8 1.6 %copy.10 = f32[4,32,256]{2,1,0:T(8,128)} copy(f32[4,32,256]{2,1,0:T(8,128)} %get-tuple-element.4) | data formatting | bytes 262144
  86.4 0.0 copy-done
  86.4 0.7 copy.11
Async XLA Ops:
  84.8 1.6 %copy-start = (bf16[1,32,2048]{2,1,0:T(8,128)(2,1)S(1)}, bf16[1,32,2048]{2,1,0:T(8,128)(2,1)}, u32[]{:S(2)}) copy-start(bf16[1,32,2048]{2,1,0:T(8,128)(2,1)} %get-tuple-element.5) | copy-start | bytes 393220

commit v5 on v4

--- a/solution.py
+++ b/solution.py
@@ -64,6 +64,13 @@
     sibling = {"c": 1 - c}
     partner = {"yl": 1 - yl}
 
+    barrier = pltpu.get_barrier_semaphore()
+    near = [{"z": lax.rem(z + 1, 8)}, {"z": lax.rem(z + 7, 8)}] + [{"yh": lax.rem(yh + o, 4)} for o in (1, 2, 3)]
+    for o in range(1, 16):
+        there = lax.rem(state * 2 + c + o, 16)
+        near.append({"yl": there // 8, "x": lax.rem(there // 2, 4), "c": lax.rem(there, 2)})
+    for device in near:
+        pl.semaphore_signal(barrier, inc=1, device_id=device, device_id_type=pl.DeviceIdType.MESH)
     own = [
         pltpu.make_async_copy(env_ref.at[0], rows.at[0, 0, c], local_sem.at[0]),
         pltpu.make_async_copy(edge_ref, pairs, local_sem.at[1]),
@@ -75,13 +82,6 @@
     for copy in own:
         copy.start()
 
-    barrier = pltpu.get_barrier_semaphore()
-    near = [{"z": lax.rem(z + 1, 8)}, {"z": lax.rem(z + 7, 8)}] + [{"yh": lax.rem(yh + o, 4)} for o in (1, 2, 3)]
-    for o in range(1, 16):
-        there = lax.rem(state * 2 + c + o, 16)
-        near.append({"yl": there // 8, "x": lax.rem(there // 2, 4), "c": lax.rem(there, 2)})
-    for device in near:
-        pl.semaphore_signal(barrier, inc=1, device_id=device, device_id_type=pl.DeviceIdType.MESH)
     own[1].wait()
     for p in (0, 1):
         edges[0, 0, c, :, 256 * p:256 * (p + 1)] = pairs[:, p, :]
@@ -208,8 +208,12 @@
 
     def send_moved(s):
         moved_copy(s, False, partner, 0).start()
-        for copy in along_x(s, False, (1, 2, 3) if s == 7 else (1, 3)):
+        for copy in along_x(s, False, (1, 3)):
             copy.start()
+        if s == 7:
+            @pl.when(c == 0)
+            def _():
+                near_x(s, False, 2).start()
 
     def send_proj(s):
         home = origin(s) == state
@@ -257,8 +261,12 @@
 
     def relay(s):
         moved_copy(s, False, partner, 0).wait_recv()
-        for copy in along_x(s, True, (1, 2, 3) if s == 7 else (1, 3)):
+        for copy in along_x(s, True, (1, 3)):
             copy.start()
+        if s == 7:
+            @pl.when(c == 0)
+            def _():
+                near_x(s, True, 2).start()
 
     def relay_far(s):
         moved_here(s, 2, 1)
@@ -273,7 +281,10 @@
             seen.add(s)
             edge_last(s)
         if u == 7:
-            moved_here(u, 2, 1)
+            @pl.when(c == 0)
+            def _():
+                moved_here(u, 2, 1)
+
         moved_here(u, 4, 2)
         site = unit_of(edges, u)[...].reshape(128, SITE)
         for p in (0, 1):
@@ -318,7 +329,7 @@
                 @pl.when(jnp.logical_or(s < 3, c == (1 if q < 2 else 0)))
                 def _():
                     passing(s, q, other).start()
-        if place == 2:
+        if place == 1:
             for copy in swap:
                 copy.start()
         if place == 5:
@@ -343,6 +354,11 @@
     last_chunks(0, (3,))
     relay(6)
     tasks(17)
+
+    @pl.when(c == 1)
+    def _():
+        relay_far(7)
+
     last_chunks(0, (2,))
     last_row(0)
     relay_far(5)

time: 87.2 us -> 86.4 us (level)
  no operation moved by 1% of the time
where the time goes in v5:
time: 86.4 us; the launch traced here: 86.3 us
  Pallas kernels  83.4 us (97%)
  local copies, waits for them, and re-layouts  2.26 us (3%)
    pallas_call x1, Pallas kernels, shards(): pl.pallas_call(kernel, out_shape=(jax.ShapeDtypeStruct((4, 32, 256), F32)...  83.4 us
    unnamed x4, local copies, waits for them, and re-layouts  2.26 us

profile of v5, /device:TPU:1, one launch (start us, length us, event | category | flops | bytes accessed | tf_op | source)
XLA Modules:
  0.0 86.3 jit_solution(17100739309891453398)
XLA Ops:
  0.6 83.4 %project_and_grow.1 = (f32[4,32,256]{2,1,0:T(8,128)}, bf16[1,32,2048]{2,1,0:T(8,128)(2,1)}) custom-call(bf16[1,32,2048]{2,1,0:T(8,128)(2,1)} %env_ref.1, bf16[1,4,32,2048]{3,2,1,0:T(8,128)(2,1)} %block_ref.1, bf16[1,2,32,2048]{3,2,1,0:T(8,128)(2,1)} %site_ref.1, bf16[32,2,256]{2,1,0:T(2,128)(2,1)} %edge_ref.1, bf16[4,32,256]{2,1,0:T(8,128)(2,1)} %current_ref.1, ...), custom_call_target="tpu_custom_call" | custom-call | tf_op jit(solution)/shard_map/project_and_grow/pallas_call | solution.py:508
  84.0 0.0 copy-start
  84.0 1.6 %copy.10 = f32[4,32,256]{2,1,0:T(8,128)} copy(f32[4,32,256]{2,1,0:T(8,128)} %get-tuple-element.4) | data formatting | bytes 262144
  85.6 0.0 copy-done
  85.6 0.7 copy.11
Async XLA Ops:
  84.0 1.6 %copy-start = (bf16[1,32,2048]{2,1,0:T(8,128)(2,1)S(1)}, bf16[1,32,2048]{2,1,0:T(8,128)(2,1)}, u32[]{:S(2)}) copy-start(bf16[1,32,2048]{2,1,0:T(8,128)(2,1)} %get-tuple-element.5) | copy-start | bytes 393220

commit v6 on v5

--- a/solution.py
+++ b/solution.py
@@ -24,10 +24,10 @@
 TASKS = {
     5: [(0, 1)],
     7: [(0, 2)],
-    8: [(0, 0), (1, 1)],
+    8: [(1, 1)],
     10: [(0, 3)],
-    11: [(0, 4), (1, 0), (1, 2), (2, 1)],
-    13: [(0, 5), (1, 3), (2, 0)],
+    11: [(0, 4), (1, 2), (2, 1)],
+    13: [(0, 5), (1, 3)],
     14: [(2, 2), (1, 4)],
     15: [(0, 6), (3, 1)],
     16: [(1, 5), (2, 3)],
@@ -332,11 +332,16 @@
         if place == 1:
             for copy in swap:
                 copy.start()
-        if place == 5:
+        if place == 4:
             own[2].wait()
             own[3].wait()
             pltpu.make_async_copy(stored.at[:, c], stored.at[:, c], s_recv).wait()
-        if place == 13:
+        for core, spots in ((1, (4, 8, 11)), (0, (8, 11, 13))):
+            if place in spots:
+                @pl.when(c == core)
+                def _():
+                    (multiply, relay, relay_far)[spots.index(place)](0)
+        if place == 12:
             last_chunks(1, (0, 1))
             last_row(1)
         tasks(place)

time: 86.4 us -> 86.4 us (level)
  no operation moved by 1% of the time
where the time goes in v6:
time: 86.4 us; the launch traced here: 86.3 us
  Pallas kernels  83.4 us (97%)
  local copies, waits for them, and re-layouts  2.26 us (3%)
    pallas_call x1, Pallas kernels, shards(): pl.pallas_call(kernel, out_shape=(jax.ShapeDtypeStruct((4, 32, 256), F32)...  83.4 us
    unnamed x4, local copies, waits for them, and re-layouts  2.26 us

profile of v6, /device:TPU:1, one launch (start us, length us, event | category | flops | bytes accessed | tf_op | source)
XLA Modules:
  0.0 86.3 jit_solution(12605818232090058712)
XLA Ops:
  0.6 83.4 %project_and_grow.1 = (f32[4,32,256]{2,1,0:T(8,128)}, bf16[1,32,2048]{2,1,0:T(8,128)(2,1)}) custom-call(bf16[1,32,2048]{2,1,0:T(8,128)(2,1)} %env_ref.1, bf16[1,4,32,2048]{3,2,1,0:T(8,128)(2,1)} %block_ref.1, bf16[1,2,32,2048]{3,2,1,0:T(8,128)(2,1)} %site_ref.1, bf16[32,2,256]{2,1,0:T(2,128)(2,1)} %edge_ref.1, bf16[4,32,256]{2,1,0:T(8,128)(2,1)} %current_ref.1, ...), custom_call_target="tpu_custom_call" | custom-call | tf_op jit(solution)/shard_map/project_and_grow/pallas_call | solution.py:513
  84.0 0.0 copy-start
  84.0 1.6 %copy.10 = f32[4,32,256]{2,1,0:T(8,128)} copy(f32[4,32,256]{2,1,0:T(8,128)} %get-tuple-element.4) | data formatting | bytes 262144
  85.6 0.0 copy-done
  85.6 0.7 copy.11
Async XLA Ops:
  84.0 1.6 %copy-start = (bf16[1,32,2048]{2,1,0:T(8,128)(2,1)S(1)}, bf16[1,32,2048]{2,1,0:T(8,128)(2,1)}, u32[]{:S(2)}) copy-start(bf16[1,32,2048]{2,1,0:T(8,128)(2,1)} %get-tuple-element.5) | copy-start | bytes 393220
